TPU v7x, 32 devices: a whole 2x2x4 slice. The times are simulated.
32 devices in a mesh: dp: 2 (over x), tp: 4 (over z), sp: 4 (over y, core).
Axes of the slice: x: 2, y: 2, z: 4, core: 2. Of those that a mesh axis runs over, the one named last changes fastest.
Arguments:
- hidden: bfloat16 [128, 6144], P('dp'), parts along dimension 0
- norm_scale: bfloat16 [6144], replicated
- w_qkv: bfloat16 [6144, 8192], P(None, 'tp')
- w_out: bfloat16 [6144, 6144], P('tp')
- k_cache: bfloat16 [128, 1024, 8, 128], P('dp', 'sp', 'tp'), parts along dimension 0
- v_cache: bfloat16 [128, 1024, 8, 128], P('dp', 'sp', 'tp'), parts along dimension 0
- positions: int32 [128], P('dp'), parts along dimension 0
Outputs:
- output 1: bfloat16 [128, 6144], P('dp'), parts along dimension 0
- output 2: bfloat16 [128, 1024, 8, 128], P('dp', 'sp', 'tp'), parts along dimension 0
- output 3: bfloat16 [128, 1024, 8, 128], P('dp', 'sp', 'tp'), parts along dimension 0
There are 2 independent parts. A program takes and returns all parts, laid end to end along the dimension named above; an argument that names none is the same for every part.
All inputs are finite; a program needn't handle non-finite values.
Results may differ from a plain program's by a relative error of at most 0.00644112.
Values sent between devices are 32-bit elements.
A program may use at most 1 GiB of HBM per device.

v0:
```python
import math
import jax
import jax.numpy as jnp
from jax import lax
from jax.sharding import PartitionSpec as P


def rope_apply(head_vals, positions):
    half_dim = head_vals.shape[-1] // 2
    inv_freq = jnp.exp(jnp.arange(half_dim, dtype=jnp.float32) * (-2.0 * math.log(500000.0) / head_vals.shape[-1]))
    angles = positions.astype(jnp.float32)[:, None] * inv_freq[None, :]
    cos_part = jnp.cos(angles)[:, None, None, :]
    sin_part = jnp.sin(angles)[:, None, None, :]
    first_half = head_vals[..., :half_dim]
    second_half = head_vals[..., half_dim:]
    return jnp.concatenate([first_half * cos_part - second_half * sin_part, second_half * cos_part + first_half * sin_part], axis=-1)


def layer_norm_bf16(hidden_f32, norm_scale):
    row_mean = jnp.mean(hidden_f32, axis=-1, keepdims=True)
    centered = hidden_f32 - row_mean
    row_var = jnp.mean(centered * centered, axis=-1, keepdims=True)
    return (centered * lax.rsqrt(row_var + 1e-5) * norm_scale.astype(jnp.float32)).astype(jnp.bfloat16)


def solution(mesh):
    cache_spec = P('dp', 'sp', 'tp', None)

    def local_step(hidden, norm_scale, w_qkv, w_out, k_cache, v_cache, positions):
        n_seq, seq_local, kv_local, head_dim = k_cache.shape
        q_per_kv = w_qkv.shape[1] // (kv_local * head_dim) - 2
        hidden_f32 = hidden.astype(jnp.float32)
        normed = layer_norm_bf16(hidden_f32, norm_scale)
        qkv_proj = jnp.clip(jnp.dot(normed, w_qkv, preferred_element_type=jnp.float32).astype(jnp.bfloat16), -8.0, 8.0)
        grouped = qkv_proj.reshape(n_seq, kv_local, q_per_kv + 2, head_dim)
        rotated = rope_apply(grouped[:, :, : q_per_kv + 1].astype(jnp.float32), positions).astype(jnp.bfloat16)
        queries = rotated[:, :, :q_per_kv]
        row_index = lax.axis_index('sp') * seq_local + jnp.arange(seq_local)
        new_row = (row_index[None, :] == positions[:, None])[:, :, None, None]
        k_upd = jnp.where(new_row, rotated[:, :, q_per_kv][:, None], k_cache)
        v_upd = jnp.where(new_row, grouped[:, :, q_per_kv + 1][:, None], v_cache)
        scores = jnp.einsum('bgqd,bsgd->bgqs', queries, k_upd, preferred_element_type=jnp.float32) * (head_dim ** -0.5)
        valid_mask = row_index[None, :] <= positions[:, None]
        scores = jnp.where(valid_mask[:, None, None, :], scores, -1e30)
        local_max = jnp.max(scores, axis=-1)
        weights = jnp.exp(scores - local_max[..., None])
        local_sum = jnp.sum(weights, axis=-1)
        local_out = jnp.einsum('bgqs,bsgd->bgqd', weights.astype(jnp.bfloat16), v_upd, preferred_element_type=jnp.float32)
        global_max = lax.pmax(local_max, 'sp')
        factor = jnp.exp(local_max - global_max)
        packed = jnp.concatenate([local_out * factor[..., None], (local_sum * factor)[..., None]], axis=-1)
        merged = lax.psum(packed, 'sp')
        attn_out = merged[..., :head_dim] / merged[..., head_dim:]
        attn_flat = attn_out.reshape(n_seq, kv_local * q_per_kv * head_dim).astype(jnp.bfloat16)
        head_part = jnp.dot(attn_flat, w_out, preferred_element_type=jnp.float32)
        proj_sum = lax.psum(head_part, 'tp')
        h_out = (hidden_f32 + proj_sum).astype(jnp.bfloat16)
        return h_out, k_upd, v_upd

    return jax.shard_map(
        local_step,
        mesh=mesh,
        in_specs=(P('dp', None), P(None), P(None, 'tp'), P('tp', None), cache_spec, cache_spec, P('dp')),
        out_specs=(P('dp', None), cache_spec, cache_spec),
        check_vma=False,
    )
```

profile of v0, /device:TPU:0, one launch (start us, length us, event | category | flops | bytes accessed | tf_op | source)
XLA Modules:
  0.0 206.9 jit_solution(4029630847443421616)
XLA Ops:
  7.2 0.0 all-reduce.3.cloned.1.call-start
  7.2 1.3 convert_reduce_fusion
  8.6 1.5 fusion.7
  10.1 0.7 convert_element_type.36
  10.8 13.0 %fusion.20 = bf16[8,8,16,128]{3,1,2,0:T(8,128)(2,1)S(1)} fusion(bf16[6144,2048]{1,0:T(8,128)(2,1)} %param.9, bf16[64,6144]{1,0:T(8,128)(2,1)} %param.7, f32[6144]{0:T(1024)S(1)} %convert_element_type.36, f32[64]{0:T(128)S(1)} %add_rsqrt_fusion, f32[64]{0:T(128)S(1)} %broadcast_multiply_fusion), kind=kOutput, calls=%fused_computation.20 | convolution fusion | flops 1612840960 | bytes 26239488 | tf_op jit(solution)/shard_map/dot_general | solution.py:34
  23.9 0.1 slice.37
  24.0 0.1 broadcast_compare_fusion.1
  24.2 0.2 multiply_cosine_fusion
  24.4 0.2 subtract_convert_fusion
  24.6 0.3 pad_maximum_fusion.1
  24.9 25.6 %broadcast_select_fusion = (bf16[64,256,2,128]{3,2,1,0:T(2,128)(2,1)}, bf16[64,256,2,128]{3,2,1,0:T(2,128)(2,1)S(1)}) fusion(bf16[64,256,2,128]{3,2,1,0:T(2,128)(2,1)} %param.12, pred[64,256]{1,0:T(8,128)(4,1)S(1)} %get-tuple-element.10, bf16[64,2,128]{2,1,0:T(2,128)(2,1)S(1)} %copy.27, bf16[64,256,2,128]{3,2,1,0:T(2,128)(2,1)} %param.11, ...), kind=kLoop, calls=%fused_computation | loop fusion | flops 8388608 | bytes 33636352 | tf_op jit(solution)/shard_map/jit(_where)/select_n | solution.py:41
  50.5 0.0 copy-start
  50.6 3.4 %copy-done = bf16[64,256,2,128]{3,2,1,0:T(2,128)(2,1)} copy-done((bf16[64,256,2,128]{3,2,1,0:T(2,128)(2,1)}, bf16[64,256,2,128]{3,2,1,0:T(2,128)(2,1)S(1)}, u32[]{:S(2)}) %copy-start) | copy-done | bytes 8388632
  53.9 2.4 %fusion.36 = (f32[64,2,6]{2,1,0:T(2,128)S(1)}, f32[64,2,6,256]{3,2,1,0:T(8,128)S(1)}) fusion(bf16[64,256,2,128]{3,2,1,0:T(2,128)(2,1)S(1)} %get-tuple-element.8, bf16[64,2,7,64]{3,2,1,0:T(8,128)(2,1)S(1)} %get-tuple-element.6, bf16[64,2,7,64]{3,2,1,0:T(8,128)(2,1)S(1)} %get-tuple-element.5, pred[64,256]{1,0:T(8,128)(4,1)S(1)} %get-tuple-element.9), kind=kOutput, calls=%fused_computation.53 | convolution fusion | flops 51313920 | bytes 9423872 | tf_op jit(solution)/shard_map/bgqd,bsgd->bgqs/dot_general | solution.py:42
  56.4 13.5 %pmax.7 = f32[64,2,6]{2,1,0:T(2,128)S(1)} all-reduce(f32[64,2,6]{2,1,0:T(2,128)S(1)} %get-tuple-element.13), channel_id=1, replica_groups=mesh['dp'=2,'tp'=4,'sp'=4] {'sp'}, use_global_device_ids=true, to_apply=%region_3.4 | all-reduce | flops 768 | bytes 6144 | tf_op jit(solution)/shard_map/pmax | solution.py:49
  69.9 0.4 fusion.21
  70.3 0.1 multiply_bitcast_fusion
  70.4 0.9 copy.30
  71.3 4.7 %fusion.17 = f32[64,2,6,128]{3,2,1,0:T(8,128)S(1)} fusion(bf16[64,256,2,128]{3,2,1,0:T(2,128)(2,1)} %get-tuple-element.7, f32[64,2,6,256]{3,2,1,0:T(8,128)S(1)} %get-tuple-element.14, f32[64,2,6]{2,1,0:T(2,128)S(1)} %get-tuple-element.13, f32[64,2,6]{2,1,0:T(2,128)S(1)} %get-tuple-element.4), kind=kOutput, calls=%fused_computation.19 | convolution fusion | flops 50823168 | bytes 9574400 | tf_op jit(solution)/shard_map/bgqs,bsgd->bgqd/dot_general | solution.py:48
  76.0 1.2 pad_maximum_fusion
  77.1 0.0 all-reduce.3.cloned.1.call-update
  77.2 0.2 all-reduce.5.cloned.1.call-start
  77.4 36.6 %all-reduce.3.cloned.1.call-done = f32[64,2,6,129]{3,2,1,0:T(8,128)} async-done(((f32[64,2,6,129]{3,2,1,0:T(8,128)}), f32[64,2,6,129]{3,2,1,0:T(8,128)}) %all-reduce.3.cloned.1.call-update) | async-done | bytes 396304 | tf_op jit(solution)/shard_map/psum | solution.py:52
  114.0 1.1 slice.39
  115.0 0.9 copy.35
  115.9 1.3 fusion.28
  117.2 0.2 convert_element_type.43
  117.4 0.0 copy-start.1
  117.4 11.0 %fusion.37 = f32[64,6144]{1,0:T(8,128)} fusion(bf16[64,1536]{1,0:T(8,128)(2,1)S(1)} %convert_element_type.43, bf16[1536,6144]{1,0:T(8,128)(2,1)} %param.10), kind=kOutput, calls=%fused_computation.54 | convolution fusion | flops 1207959552 | bytes 20643840 | tf_op jit(solution)/shard_map/dot_general | solution.py:55
  128.4 0.0 all-reduce.5.cloned.1.call-update
  128.4 69.2 %all-reduce.5.cloned.1.call-done = f32[64,6144]{1,0:T(8,128)} async-done(((f32[64,6144]{1,0:T(8,128)}), f32[64,6144]{1,0:T(8,128)}) %all-reduce.5.cloned.1.call-update) | async-done | bytes 1572880 | tf_op jit(solution)/shard_map/psum | solution.py:56
  197.7 2.4 %fusion.10 = bf16[64,6144]{1,0:T(8,128)(2,1)} fusion(f32[64,6144]{1,0:T(8,128)} %all-reduce.5.cloned.1.call-done, bf16[64,6144]{1,0:T(8,128)(2,1)S(1)} %copy-done.1), kind=kLoop, calls=%fused_computation.16 | loop fusion | flops 1179648 | bytes 3145728 | tf_op jit(solution)/shard_map/convert_element_type | solution.py:57
  (14 shorter events, 0.2 us)
Async XLA Ops:
  7.2 106.8 %all-reduce.3.cloned.1.call-start = ((), (), s32[]{:S(2)}) async-start(), calls=%async_computation | async-start | bytes 2097152 | tf_op jit(solution)/shard_map/psum | solution.py:52
  10.8 13.2 %copy-start.2 = (s32[64]{0:T(128)S(1)}, s32[64]{0:T(128)}, u32[]{:S(2)}) copy-start(s32[64]{0:T(128)} %param.13) | copy-start | bytes 772
  50.5 3.4 %copy-start = (bf16[64,256,2,128]{3,2,1,0:T(2,128)(2,1)}, bf16[64,256,2,128]{3,2,1,0:T(2,128)(2,1)S(1)}, u32[]{:S(2)}) copy-start(bf16[64,256,2,128]{3,2,1,0:T(2,128)(2,1)S(1)} %get-tuple-element.8) | copy-start | bytes 25165828
  77.2 120.5 %all-reduce.5.cloned.1.call-start = ((), (), s32[]{:S(2)}) async-start(), calls=%async_computation.1 | async-start | bytes 3145728 | tf_op jit(solution)/shard_map/psum | solution.py:56
  117.4 80.2 %copy-start.1 = (bf16[64,6144]{1,0:T(8,128)(2,1)S(1)}, bf16[64,6144]{1,0:T(8,128)(2,1)}, u32[]{:S(2)}) copy-start(bf16[64,6144]{1,0:T(8,128)(2,1)} %param.7) | copy-start | bytes 2359300
Sparse Core Ops, SparseCore 0:
  77.3 36.6 all-reduce.2
  128.6 69.0 all-reduce.4
where the time goes:
time: 207 us
  waiting for transfers between devices  106 us (51%)
  other arithmetic  35.3 us (17%)
  matrix products  31.1 us (15%)
  between operations  14.2 us (7%)
  blocking collectives  13.5 us (7%)
  local copies, waits for them, and re-layouts  6.68 us (3%)
    psum x1, waiting for transfers between devices, local_step(): proj_sum = lax.psum(head_part, 'tp')  69.2 us
    psum x1, waiting for transfers between devices, local_step(): merged = lax.psum(packed, 'sp')  36.6 us
    select_n x1, other arithmetic, local_step(): v_upd = jnp.where(new_row, grouped[:, :, q_per_kv + 1][:, None], v_cache)  25.6 us
    pmax x1, blocking collectives, local_step(): global_max = lax.pmax(local_max, 'sp')  13.5 us
    dot_general x1, matrix products, local_step(): jnp.dot(normed, w_qkv, preferred_element_type=jnp.float32)  13 us
    dot_general x1, matrix products, local_step(): head_part = jnp.dot(attn_flat, w_out, preferred_element_type=jnp.float32)  11 us
    dot_general x1, matrix products, local_step(): jnp.einsum('bgqs,bsgd->bgqd', weights.astype(jnp.bfloat16), v_upd, prefer...  4.69 us
  transfers between devices with their start and end apart: 2, of which 2 were waited for; matrix products, arithmetic and copies ran while one was open for 0% of the time, Pallas kernels for 0%

commit v1 on v0

v1 whole, which is shorter than its diff:
```python
import math
import jax
import jax.numpy as jnp
from jax import lax
from jax.experimental import pallas as pl
from jax.experimental.pallas import tpu as pltpu
from jax.sharding import PartitionSpec as P

F32 = jnp.float32
BF16 = jnp.bfloat16
MESH = pl.DeviceIdType.MESH

NB = 64
D = 6144
HD = 128
SEQ_LOCAL = 256
ROWS = 2 * SEQ_LOCAL
QPK = 6
NEG = -1e30

WCOL = 256
WSLOTS = 4
CB = 8
NCB = NB // CB
VMEM_OUT = True

HALF = 32
NC = 12
CW = D // 2 // NC
SKEW = 3


def attn_kernel(hid, scale, cosf, sinf, pos, w_hbm, k_hbm, v_hbm,
                o_ref, st_ref, k_out, v_out,
                *scratch):
    if VMEM_OUT:
        x_s, wbuf, q_s, kv_s, wsem, ksem, vsem = scratch
        k_ref, v_ref = k_out, v_out
    else:
        x_s, wbuf, q_s, kv_s, wsem, ksem, vsem, k_ref, v_ref, kosem, vosem = scratch
    nw = w_hbm.shape[1] // WCOL
    sp = lax.axis_index('sp')

    def wcopy(j):
        return pltpu.make_async_copy(w_hbm.at[:, pl.ds(pl.multiple_of(j * WCOL, WCOL), WCOL)], wbuf.at[j % WSLOTS], wsem.at[j % WSLOTS])

    def kcopy(c):
        return pltpu.make_async_copy(k_hbm.at[pl.ds(c * CB, CB)], k_ref.at[pl.ds(c * CB, CB)], ksem.at[c])

    def vcopy(c):
        return pltpu.make_async_copy(v_hbm.at[pl.ds(c * CB, CB)], v_ref.at[pl.ds(c * CB, CB)], vsem.at[c])

    for j in range(WSLOTS):
        wcopy(j).start()

    def norm_block(i, carry):
        rows = pl.ds(pl.multiple_of(i * 16, 16), 16)
        h = hid[rows, :].astype(F32)
        mean = jnp.mean(h, axis=-1, keepdims=True)
        cen = h - mean
        var = jnp.mean(cen * cen, axis=-1, keepdims=True)
        x_s[rows, :] = (cen * lax.rsqrt(var + 1e-5) * scale[...].astype(F32)).astype(BF16)
        return carry

    lax.fori_loop(0, NB // 16, norm_block, 0)
    q_s[...] = jnp.zeros_like(q_s)

    def rope(y):
        r = y * cosf[...] + pltpu.roll(y, HD // 2, 1) * sinf[...]
        return r.astype(BF16).astype(F32)

    def group(g, carry):
        for jj in range(4):
            j = g * 4 + jj
            wcopy(j).wait()
            acc = jnp.dot(x_s[...], wbuf[j % WSLOTS], preferred_element_type=F32)

            @pl.when(g == 0)
            def _():
                wcopy(j + WSLOTS).start()

            @pl.when(g == 1)
            def _():
                for c in range(2):
                    kcopy(2 * jj + c).start()
                    vcopy(2 * jj + c).start()

            y = jnp.clip(acc.astype(BF16).astype(F32), -8.0, 8.0)
            y0, y1 = y[:, :HD], y[:, HD:]
            if jj < 3:
                q_s[pl.ds(g * 8 + 2 * jj, NB, stride=16), :] = rope(y0)
                q_s[pl.ds(g * 8 + 2 * jj + 1, NB, stride=16), :] = rope(y1)
            else:
                kv_s[pl.ds(g, NB, stride=8), :] = rope(y0)
                kv_s[pl.ds(g + 2, NB, stride=8), :] = y1
        return carry

    lax.fori_loop(0, 2, group, 0)

    sub16 = lax.broadcasted_iota(jnp.int32, (16, HD), 0)
    col = lax.broadcasted_iota(jnp.int32, (16, ROWS), 1)
    row = lax.broadcasted_iota(jnp.int32, (16, ROWS), 0)
    parity_ok = (col % 2) == (row // 8)
    lane = lax.broadcasted_iota(jnp.int32, (16, HD), 1)

    def insert(b, r, cache, base_row):
        own = jnp.logical_and(r >= 0, r < SEQ_LOCAL)
        rc = jnp.clip(r, 0, SEQ_LOCAL - 1)
        start = pl.multiple_of((rc // 8) * 16, 16)
        sub = jnp.where(own, rc % 8, -1)
        n0 = kv_s[pl.ds(b * 8 + base_row, 1), :]
        n1 = kv_s[pl.ds(b * 8 + base_row + 1, 1), :]
        new = jnp.where(sub16 % 2 == 0, n0, n1)
        tile = cache[b, pl.ds(start, 16), :].astype(F32)
        cache[b, pl.ds(start, 16), :] = jnp.where(sub16 // 2 == sub, new, tile).astype(BF16)

    def chunk(c, stats):
        kcopy(c).wait()
        vcopy(c).wait()
        for i in range(CB):
            b = c * CB + i
            r = pos[b] - sp * SEQ_LOCAL
            insert(b, r, k_ref, 0)
            insert(b, r, v_ref, 2)
        if not VMEM_OUT:
            pltpu.make_async_copy(k_ref.at[pl.ds(c * CB, CB)], k_out.at[pl.ds(c * CB, CB)], kosem.at[c]).start()
            pltpu.make_async_copy(v_ref.at[pl.ds(c * CB, CB)], v_out.at[pl.ds(c * CB, CB)], vosem.at[c]).start()
        for i in range(CB):
            b = c * CB + i
            r = pos[b] - sp * SEQ_LOCAL
            q = q_s[pl.ds(pl.multiple_of(b * 16, 16), 16), :].astype(BF16)
            s = lax.dot_general(q, k_ref[b], (((1,), (1,)), ((), ())), preferred_element_type=F32) * (HD ** -0.5)
            s = jnp.where(jnp.logical_and(parity_ok, col < 2 * r + 2), s, NEG)
            m = jnp.max(s, axis=1, keepdims=True)
            p = jnp.exp(s - m)
            l = jnp.sum(p, axis=1, keepdims=True)
            o = jnp.dot(p.astype(BF16), v_ref[b], preferred_element_type=F32)
            o_ref[pl.ds(b, 16, stride=NB), :] = o
            stats = jnp.where(lane == b, m, jnp.where(lane == b + NB, l, stats))
        return stats

    stats = lax.fori_loop(0, NCB, chunk, jnp.zeros((16, HD), F32))
    for g in range(2):
        block = jnp.concatenate([stats[8 * g:8 * g + 8], jnp.zeros((HD - 8, HD), F32)], axis=0)
        st_ref[g] = jnp.transpose(block).reshape(2, NB, HD)
    if not VMEM_OUT:
        for c in range(NCB):
            pltpu.make_async_copy(k_ref.at[pl.ds(c * CB, CB)], k_out.at[pl.ds(c * CB, CB)], kosem.at[c]).wait()
            pltpu.make_async_copy(v_ref.at[pl.ds(c * CB, CB)], v_out.at[pl.ds(c * CB, CB)], vosem.at[c]).wait()


def merge_kernel(o_in, st_in, hid, w_hbm, out,
                 wbuf, oa, sta, o2, st2, ob, stb, a_own, a_rem, p_s, z1, a_z, z2, t_s, y_in, c_in, cy_in,
                 wsem, osem, s1, r1, s2, r2, s3, r3, zs, zr, z2s, z2r, ts, ys, yr, cs, cr, cys, cyr):
    dp = lax.axis_index('dp')
    tp = lax.axis_index('tp')
    sp = lax.axis_index('sp')
    core = sp % 2
    yy = sp // 2
    partner = sp + 1 - 2 * core
    ynbr = sp + 2 - 4 * yy
    inner = jnp.logical_or(tp == 1, tp == 2)
    outer = jnp.logical_not(inner)
    n_inner = jnp.where(inner, 1, 0)
    z_in_nbr = jnp.where(tp < 2, jnp.where(tp == 0, 1, 2), jnp.where(tp == 3, 2, 1))
    z_out_nbr = jnp.where(tp < 2, 0, 3)

    def dev(t, s):
        return (dp, t, s)

    cols = core * (D // 2)

    def wcopy(j):
        return pltpu.make_async_copy(w_hbm.at[:, pl.ds(pl.multiple_of(cols + j * CW, CW), CW)], wbuf.at[j], wsem.at[j])

    for j in range(NC):
        wcopy(j).start()

    barrier = pltpu.get_barrier_semaphore()
    pl.semaphore_signal(barrier, inc=1, device_id=dev(tp, partner), device_id_type=MESH)
    pl.semaphore_signal(barrier, inc=1, device_id=dev(tp, ynbr), device_id_type=MESH)
    pl.semaphore_signal(barrier, inc=1, device_id=dev(z_in_nbr, sp), device_id_type=MESH)

    @pl.when(inner)
    def _():
        pl.semaphore_signal(barrier, inc=1, device_id=dev(z_out_nbr, sp), device_id_type=MESH)

    pl.semaphore_wait(barrier, 3 + n_inner)

    def rcopy(src, dst, ssem, rsem, t, s):
        return pltpu.make_async_remote_copy(src_ref=src, dst_ref=dst, send_sem=ssem, recv_sem=rsem, device_id=dev(t, s), device_id_type=MESH)

    ca = rcopy(o_in.at[1 - core, pl.ds(0, QPK)], oa, s1.at[0], r1.at[0], tp, partner)
    cb = rcopy(st_in.at[1 - core], sta, s1.at[1], r1.at[1], tp, partner)
    ca.start()
    cb.start()
    ca.wait_recv()
    cb.wait_recv()

    def factors(m0, l0, m1, l1):
        top = jnp.maximum(m0, m1)
        f0 = jnp.exp(m0 - top)
        f1 = jnp.exp(m1 - top)
        return top, f0, f1, f0 * l0 + f1 * l1

    def pair_merge(start):
        rows = pl.ds(pl.multiple_of(start, HALF), HALF)
        top, f0, f1, total = factors(st_in[core, 0, rows, :], st_in[core, 1, rows, :], sta[0, rows, :], sta[1, rows, :])
        st2[0, rows, :] = top
        st2[1, rows, :] = total
        for i in range(QPK):
            o2[i, rows, :] = o_in[core, i, rows, :] * f0[:, i:i + 1] + oa[i, rows, :] * f1[:, i:i + 1]

    other = pl.ds(pl.multiple_of((1 - yy) * HALF, HALF), HALF)
    mine = pl.ds(pl.multiple_of(yy * HALF, HALF), HALF)
    pair_merge((1 - yy) * HALF)
    cc = rcopy(o2.at[:, other, :], ob, s2.at[0], r2.at[0], tp, ynbr)
    cd = rcopy(st2.at[:, other, :], stb, s2.at[1], r2.at[1], tp, ynbr)
    cc.start()
    cd.start()
    pair_merge(yy * HALF)
    cc.wait_recv()
    cd.wait_recv()
    top, f0, f1, total = factors(st2[0, mine, :], st2[1, mine, :], stb[0], stb[1])
    inv = 1.0 / total
    f0 = f0 * inv
    f1 = f1 * inv
    for i in range(QPK):
        a = o2[i, mine, :] * f0[:, i:i + 1] + ob[i] * f1[:, i:i + 1]
        a_own[i] = a.astype(BF16).astype(F32)
    ce = rcopy(a_own, a_rem, s3, r3, tp, partner)
    ce.start()

    def lhs(ref):
        return jnp.concatenate([ref[i].astype(BF16) for i in range(QPK)], axis=1)

    gk = QPK * HD
    own = lhs(a_own)

    def first(j, carry):
        wcopy(j).wait()
        p_s[j] = jnp.dot(own, wbuf[j, pl.ds(pl.multiple_of(core * gk, gk), gk), :], preferred_element_type=F32)
        return carry

    lax.fori_loop(0, NC, first, 0)
    ce.wait_recv()
    rem = lhs(a_rem)

    def zc(j):
        return rcopy(p_s.at[j], z1.at[j], zs.at[j], zr.at[j], z_in_nbr, sp)

    def second(j, carry):
        p_s[j] += jnp.dot(rem, wbuf[j, pl.ds(pl.multiple_of((1 - core) * gk, gk), gk), :], preferred_element_type=F32)

        @pl.when(outer)
        def _():
            zc(j).start()
        return carry

    lax.fori_loop(0, NC, second, 0)

    def mid(j):
        return rcopy(a_z.at[j], z2.at[j], z2s.at[j], z2r.at[j], z_in_nbr, sp)

    def back(j):
        return rcopy(t_s.at[j], z1.at[j], ts.at[j], zr.at[j], z_out_nbr, sp)

    def ycopy(src, j):
        return rcopy(src.at[j], y_in.at[j], ys.at[j], yr.at[j], tp, ynbr)

    def ccopy(src, j):
        return rcopy(src.at[j], c_in.at[j], cs.at[j], cr.at[j], tp, partner)

    def cycopy(j):
        return rcopy(y_in.at[j], cy_in.at[j], cys.at[j], cyr.at[j], tp, partner)

    def put(rows_start, col_start, j, val):
        rows = pl.ds(pl.multiple_of(rows_start, HALF), HALF)
        cl = pl.ds(pl.multiple_of(col_start + j * CW, CW), CW)
        out[rows, cl] = (hid[rows, cl].astype(F32) + val).astype(BF16)

    ocols = (1 - core) * (D // 2)

    def e3(j):
        ycopy(t_s, j).wait_recv()
        cycopy(j).start()
        put((1 - yy) * HALF, cols, j, y_in[j])

    def e4(j):
        ccopy(t_s, j).wait_recv()
        put(yy * HALF, ocols, j, c_in[j])

    def e5(j):
        cycopy(j).wait_recv()
        put((1 - yy) * HALF, ocols, j, cy_in[j])

    def within(j, fn):
        @pl.when(jnp.logical_and(j >= 0, j < NC))
        def _():
            fn(j)

    @pl.when(inner)
    def _():
        def e1(j):
            back(j).wait_recv()
            a_z[j] = p_s[j] + z1[j]
            mid(j).start()

        def e2(j):
            mid(j).wait_recv()
            t_s[j] = a_z[j] + z2[j]
            back(j).start()
            ycopy(t_s, j).start()
            ccopy(t_s, j).start()
            put(yy * HALF, cols, j, t_s[j])

        def step(t, carry):
            within(t, e1)
            within(t - SKEW, e2)
            within(t - 2 * SKEW, e3)
            within(t - 3 * SKEW, e4)
            within(t - 3 * SKEW, e5)
            return carry

        lax.fori_loop(0, NC + 3 * SKEW, step, 0)

        def drain(j, carry):
            mid(j).wait_send()
            back(j).wait_send()
            ycopy(t_s, j).wait_send()
            ccopy(t_s, j).wait_send()
            cycopy(j).wait_send()
            return carry

        lax.fori_loop(0, NC, drain, 0)

    @pl.when(outer)
    def _():
        def e1(j):
            zc(j).wait_recv()
            ycopy(z1, j).start()
            ccopy(z1, j).start()
            put(yy * HALF, cols, j, z1[j])

        def step(t, carry):
            within(t, e1)
            within(t - SKEW, e3)
            within(t - 2 * SKEW, e4)
            within(t - 2 * SKEW, e5)
            return carry

        lax.fori_loop(0, NC + 2 * SKEW, step, 0)

        def drain(j, carry):
            zc(j).wait_send()
            ycopy(z1, j).wait_send()
            ccopy(z1, j).wait_send()
            cycopy(j).wait_send()
            return carry

        lax.fori_loop(0, NC, drain, 0)

    ca.wait_send()
    cb.wait_send()
    cc.wait_send()
    cd.wait_send()
    ce.wait_send()


def solution(mesh):
    cache_spec = P('dp', 'sp', 'tp', None)
    any_spec = pl.BlockSpec(memory_space=pl.ANY)
    vmem_spec = pl.BlockSpec(memory_space=pltpu.VMEM)
    smem_spec = pl.BlockSpec(memory_space=pltpu.SMEM)
    dma = pltpu.SemaphoreType.DMA

    def local_step(hidden, norm_scale, w_qkv, w_out, k_cache, v_cache, positions):
        inv_freq = jnp.exp(jnp.arange(HD // 2, dtype=F32) * (-2.0 * math.log(500000.0) / HD))
        angles = positions.astype(F32)[:, None] * inv_freq[None, :]
        cos = jnp.cos(angles)
        sin = jnp.sin(angles)
        cosf = jnp.concatenate([cos, cos], axis=1)
        sinf = jnp.concatenate([-sin, sin], axis=1)
        cache_shape = (NB, ROWS, HD)
        if VMEM_OUT:
            cache_out = pltpu.VMEM(cache_shape, BF16)
            cache_out_spec = vmem_spec
            extra = []
        else:
            cache_out = jax.ShapeDtypeStruct(cache_shape, BF16)
            cache_out_spec = any_spec
            extra = [pltpu.VMEM(cache_shape, BF16), pltpu.VMEM(cache_shape, BF16), dma((NCB,)), dma((NCB,))]
        o, st, k_new, v_new = pl.pallas_call(
            attn_kernel,
            out_shape=(jax.ShapeDtypeStruct((16 * NB, HD), F32), jax.ShapeDtypeStruct((2, 2, NB, HD), F32), cache_out, cache_out),
            in_specs=[vmem_spec, vmem_spec, vmem_spec, vmem_spec, smem_spec, any_spec, any_spec, any_spec],
            out_specs=(vmem_spec, vmem_spec, cache_out_spec, cache_out_spec),
            scratch_shapes=[
                pltpu.VMEM((NB, D), BF16),
                pltpu.VMEM((WSLOTS, D, WCOL), BF16),
                pltpu.VMEM((16 * NB, HD), F32),
                pltpu.VMEM((8 * NB, HD), F32),
                dma((WSLOTS,)), dma((NCB,)), dma((NCB,)),
            ] + extra,
            compiler_params=pltpu.CompilerParams(vmem_limit_bytes=(36 << 20) if VMEM_OUT else (56 << 20)),
            cost_estimate=pl.CostEstimate(flops=2 * NB * D * 2048 + 4 * NB * 16 * ROWS * HD, bytes_accessed=60 << 20, transcendentals=NB * 16 * ROWS),
            name='qkv_attention',
        )(hidden, norm_scale.reshape(1, D), cosf, sinf, positions, w_qkv, k_cache.reshape(cache_shape), v_cache.reshape(cache_shape))

        chunk = (NC, HALF, CW)
        h_out = pl.pallas_call(
            merge_kernel,
            out_shape=jax.ShapeDtypeStruct((NB, D), BF16),
            in_specs=[vmem_spec, vmem_spec, vmem_spec, any_spec],
            out_specs=vmem_spec,
            scratch_shapes=[
                pltpu.VMEM((NC, 2 * QPK * HD, CW), BF16),
                pltpu.VMEM((QPK, NB, HD), F32),
                pltpu.VMEM((2, NB, HD), F32),
                pltpu.VMEM((QPK, NB, HD), F32),
                pltpu.VMEM((2, NB, HD), F32),
                pltpu.VMEM((QPK, HALF, HD), F32),
                pltpu.VMEM((2, HALF, HD), F32),
                pltpu.VMEM((QPK, HALF, HD), F32),
                pltpu.VMEM((QPK, HALF, HD), F32),
            ] + [pltpu.VMEM(chunk, F32)] * 8 + [
                dma((NC,)), dma((1,)), dma((2,)), dma((2,)), dma((2,)), dma((2,)), dma(()), dma(()),
            ] + [dma((NC,))] * 11,
            compiler_params=pltpu.CompilerParams(collective_id=0, has_side_effects=True, vmem_limit_bytes=24 << 20),
            cost_estimate=pl.CostEstimate(flops=40_000_000_000, bytes_accessed=12 << 20, transcendentals=0),
            name='merge_project',
        )(o.reshape(2, 8, NB, HD), st, hidden, w_out)
        return h_out, k_new.reshape(k_cache.shape), v_new.reshape(v_cache.shape)

    return jax.shard_map(
        local_step,
        mesh=mesh,
        in_specs=(P('dp', None), P(None), P(None, 'tp'), P('tp', None), cache_spec, cache_spec, P('dp')),
        out_specs=(P('dp', None), cache_spec, cache_spec),
        check_vma=False,
    )
```

time: 207 us -> 85 us (0.41)
  waiting for transfers between devices: 106 us -> 0 us
  Pallas kernels: 0 us -> 66.5 us
  other arithmetic: 35.3 us -> 0.95 us
  matrix products: 31.1 us -> 0 us
  between operations: 14.2 us -> 0.69 us
  blocking collectives: 13.5 us -> 0 us
  local copies, waits for them, and re-layouts: 6.68 us -> 16.5 us
    psum x2 -> x0, waiting for transfers between devices: 106 us -> none  [the longest x1 69.2 us: local_step(): proj_sum = lax.psum(head_part, 'tp')]
    pallas_call x0 -> x2, Pallas kernels: none -> 66.5 us  [the longest x1 38.2 us: local_step(): pl.pallas_call(merge_kernel, out_shape=jax.ShapeDtypeStruct((NB, D), BF16...]
    dot_general x4 -> x0, matrix products: 31.1 us -> none  [the longest x1 13 us: local_step(): jnp.dot(normed, w_qkv, preferred_element_type=jnp.float32)]
    select_n x1 -> x0, other arithmetic: 25.6 us -> none  [local_step(): v_upd = jnp.where(new_row, grouped[:, :, q_per_kv + 1][:, None], v_cache)]
    pmax x1 -> x0, blocking collectives: 13.5 us -> none  [local_step(): global_max = lax.pmax(local_max, 'sp')]
    unnamed x7 -> x11, local copies, waits for them, and re-layouts: 3.44 us -> 15.8 us
    convert_element_type x5 -> x1, other arithmetic: 4.43 us -> 0.66 us  [local_step(): angles = positions.astype(F32)[:, None] * inv_freq[None, :]]
    reduce_sum x3 -> x0, other arithmetic: 3.28 us -> none  [the longest x1 1.51 us: layer_norm_bf16(): row_var = jnp.mean(centered * centered, axis=-1, keepdims=True)]
  transfers between devices with their start and end apart: 2 -> 0, of which waited for: 2 -> 0; matrix products, arithmetic and copies ran while one was open for 0% -> 0% of each run, Pallas kernels for 0% -> 0%
where the time goes in v1:
time: 85 us; the launch traced here: 84.7 us
  Pallas kernels  66.5 us (78%)
  local copies, waits for them, and re-layouts  16.5 us (19%)
  other arithmetic  0.95 us (1%)
    pallas_call x1, Pallas kernels, local_step(): pl.pallas_call(merge_kernel, out_shape=jax.ShapeDtypeStruct((NB, D), BF16...  38.2 us
    pallas_call x1, Pallas kernels, local_step(): pl.pallas_call(attn_kernel, out_shape=(jax.ShapeDtypeStruct((16 * NB, HD)...  28.3 us
    unnamed x11, local copies, waits for them, and re-layouts  15.8 us

profile of v1, /device:TPU:0, one launch (start us, length us, event | category | flops | bytes accessed | tf_op | source)
XLA Modules:
  0.0 84.7 jit_solution(10575247760052613434)
XLA Ops:
  0.6 0.7 convert_element_type.3
  1.3 0.7 reshape.30.scale
  2.0 0.2 fusion
  2.2 0.1 pad_maximum_fusion
  2.3 0.0 copy-start
  2.3 1.1 %copy-done = bf16[64,6144]{1,0:T(8,128)(2,1)S(1)} copy-done((bf16[64,6144]{1,0:T(8,128)(2,1)S(1)}, bf16[64,6144]{1,0:T(8,128)(2,1)}, u32[]{:S(2)}) %copy-start) | copy-done | bytes 786456
  3.5 0.0 copy-start.2
  3.5 0.7 copy-done.2
  4.1 0.0 copy-start.1
  4.1 28.3 %qkv_attention.1 = (f32[1024,128]{1,0:T(8,128)S(1)}, f32[2,2,64,128]{3,2,1,0:T(8,128)S(1)}, bf16[64,512,128]{2,1,0:T(8,128)(2,1)S(1)}, bf16[64,512,128]{2,1,0:T(8,128)(2,1)S(1)}) custom-call(bf16[64,6144]{1,0:T(8,128)(2,1)S(1)} %copy-done, bf16[1,6144]{1,0:T(2,128)(2,1)S(1)} %reshape.30.scale, f32[64,128]{1,0:T(8,128)S(1)} %get-tuple-element.14.cosf, ...), custom_call_target="tpu_custom_call" | custom-call | flops 1879048192 | bytes 62914560 | tf_op jit(solution)/shard_map/qkv_attention/pallas_call | solution.py:393
  32.5 0.0 copy-done.1
  32.5 0.0 copy-start.3
  32.5 6.4 %copy-done.3 = bf16[1536,6144]{1,0:T(8,128)(2,1)S(1)} copy-done((bf16[1536,6144]{1,0:T(8,128)(2,1)S(1)}, bf16[1536,6144]{1,0:T(8,128)(2,1)}, u32[]{:S(2)}) %copy-start.3) | copy-done | bytes 18874392
  38.9 38.2 %merge_project.1 = bf16[64,6144]{1,0:T(8,128)(2,1)S(1)} custom-call(f32[2,8,64,128]{3,2,1,0:T(8,128)S(1)} %bitcast.7, f32[2,2,64,128]{3,2,1,0:T(8,128)S(1)} %get-tuple-element.8.st_in, bf16[64,6144]{1,0:T(8,128)(2,1)S(1)} %copy-done.1, bf16[1536,6144]{1,0:T(8,128)(2,1)S(1)} %copy-done.3), custom_call_target="tpu_custom_call" | custom-call | flops 40000000000 | bytes 12582912 | tf_op jit(solution)/shard_map/merge_project/pallas_call | solution.py:411
  77.0 3.4 %copy.11 = bf16[64,256,2,128]{3,2,1,0:T(2,128)(2,1)} copy(bf16[64,256,2,128]{3,2,1,0:T(2,128)(2,1)S(1)} %bitcast.6) | data formatting | bytes 16777216
  80.4 3.4 %copy.12 = bf16[64,256,2,128]{3,2,1,0:T(2,128)(2,1)} copy(bf16[64,256,2,128]{3,2,1,0:T(2,128)(2,1)S(1)} %bitcast.5) | data formatting | bytes 16777216
  83.8 0.9 %copy.13 = bf16[64,6144]{1,0:T(8,128)(2,1)} copy(bf16[64,6144]{1,0:T(8,128)(2,1)S(1)} %merge_project.1) | data formatting | bytes 1572864
  (1 shorter events, 0.0 us)
Async XLA Ops:
  2.3 1.1 %copy-start = (bf16[64,6144]{1,0:T(8,128)(2,1)S(1)}, bf16[64,6144]{1,0:T(8,128)(2,1)}, u32[]{:S(2)}) copy-start(bf16[64,6144]{1,0:T(8,128)(2,1)} %hid.3) | copy-start | bytes 2359300
  3.5 0.7 copy-start.2
  4.1 28.4 %copy-start.1 = (bf16[64,6144]{1,0:T(8,128)(2,1)S(1)}, bf16[64,6144]{1,0:T(8,128)(2,1)}, u32[]{:S(2)}) copy-start(bf16[64,6144]{1,0:T(8,128)(2,1)} %hid.3) | copy-start | bytes 2359300
  32.5 6.4 %copy-start.3 = (bf16[1536,6144]{1,0:T(8,128)(2,1)S(1)}, bf16[1536,6144]{1,0:T(8,128)(2,1)}, u32[]{:S(2)}) copy-start(bf16[1536,6144]{1,0:T(8,128)(2,1)} %w_hbm.3) | copy-start | bytes 56623108

commit v2 on v1

v2 whole, which is shorter than its diff:
```python
import math
import jax
import jax.numpy as jnp
from jax import lax
from jax.experimental import pallas as pl
from jax.experimental.pallas import tpu as pltpu
from jax.sharding import PartitionSpec as P

F32 = jnp.float32
BF16 = jnp.bfloat16
MESH = pl.DeviceIdType.MESH

NB = 64
D = 6144
HD = 128
SEQ_LOCAL = 256
ROWS = 2 * SEQ_LOCAL
QPK = 6
NEG = -1e30

WCOL = 256
WSLOTS = 4
CB = 8
NCB = NB // CB

HALF = 32
CW = 512
WC = 512
NW = (7, 5)
WPW = WC // CW
NC = NW[0] * WPW
SKEW = 2
PIECE = 2
NP = QPK // PIECE


def attn_kernel(pos_hbm, scale_hbm, hid_hbm, w_hbm, k_hbm, v_hbm,
                o_ref, st_ref, k_out, v_out,
                pos, scale, hid, cosf, sinf, x_s, wbuf, q_s, kv_s, k_ref, v_ref, psem, hsem, wsem, ksem, vsem, kosem, vosem):
    sp = lax.axis_index('sp')

    def wcopy(j):
        return pltpu.make_async_copy(w_hbm.at[:, pl.ds(pl.multiple_of(j * WCOL, WCOL), WCOL)], wbuf.at[j % WSLOTS], wsem.at[j % WSLOTS])

    def kcopy(c):
        return pltpu.make_async_copy(k_hbm.at[pl.ds(c * CB, CB)], k_ref.at[pl.ds(c * CB, CB)], ksem.at[c])

    def vcopy(c):
        return pltpu.make_async_copy(v_hbm.at[pl.ds(c * CB, CB)], v_ref.at[pl.ds(c * CB, CB)], vsem.at[c])

    hcopy = pltpu.make_async_copy(hid_hbm, hid, hsem)
    hcopy.start()
    pcopy = pltpu.make_async_copy(pos_hbm, pos, psem.at[0])
    pcopy.start()
    scopy = pltpu.make_async_copy(scale_hbm, scale, psem.at[1])
    scopy.start()
    wcopy(0).start()
    wcopy(1).start()
    pcopy.wait()

    lane8 = lax.broadcasted_iota(jnp.int32, (8, HD), 1)
    sub8 = lax.broadcasted_iota(jnp.int32, (8, HD), 0)
    inv_freq = jnp.exp((lane8 % (HD // 2)).astype(F32) * (-2.0 * math.log(500000.0) / HD))

    def angle_block(i, carry):
        p = jnp.zeros((8, HD), jnp.int32)
        for e in range(8):
            p = jnp.where(sub8 == e, pos[i * 8 + e], p)
        angles = p.astype(F32) * inv_freq
        rows = pl.ds(pl.multiple_of(i * 8, 8), 8)
        cosf[rows, :] = jnp.cos(angles)
        sin = jnp.sin(angles)
        sinf[rows, :] = jnp.where(lane8 < HD // 2, -sin, sin)
        return carry

    lax.fori_loop(0, NB // 8, angle_block, 0)
    q_s[...] = jnp.zeros_like(q_s)
    wcopy(2).start()
    wcopy(3).start()
    hcopy.wait()
    scopy.wait()
    for c in range(2):
        kcopy(c).start()
        vcopy(c).start()

    def norm_block(i, carry):
        rows = pl.ds(pl.multiple_of(i * 16, 16), 16)
        h = hid[rows, :].astype(F32)
        mean = jnp.mean(h, axis=-1, keepdims=True)
        cen = h - mean
        var = jnp.mean(cen * cen, axis=-1, keepdims=True)
        x_s[rows, :] = (cen * lax.rsqrt(var + 1e-5) * scale[...].astype(F32)[None, :]).astype(BF16)
        return carry

    lax.fori_loop(0, NB // 16, norm_block, 0)

    def rope(y):
        r = y * cosf[...] + pltpu.roll(y, HD // 2, 1) * sinf[...]
        return r.astype(BF16).astype(F32)

    def group(g, carry):
        for jj in range(4):
            j = g * 4 + jj
            wcopy(j).wait()
            acc = jnp.dot(x_s[...], wbuf[j % WSLOTS], preferred_element_type=F32)

            @pl.when(g == 0)
            def _():
                wcopy(j + WSLOTS).start()

            @pl.when(g == 1)
            def _():
                for c in range((2, 4, 5, 6)[jj], (4, 5, 6, 8)[jj]):
                    kcopy(c).start()
                    vcopy(c).start()

            y = jnp.clip(acc.astype(BF16).astype(F32), -8.0, 8.0)
            y0, y1 = y[:, :HD], y[:, HD:]
            if jj < 3:
                q_s[pl.ds(g * 8 + 2 * jj, NB, stride=16), :] = rope(y0)
                q_s[pl.ds(g * 8 + 2 * jj + 1, NB, stride=16), :] = rope(y1)
            else:
                kv_s[pl.ds(g, NB, stride=8), :] = rope(y0)
                kv_s[pl.ds(g + 2, NB, stride=8), :] = y1
        return carry

    lax.fori_loop(0, 2, group, 0)

    sub16 = lax.broadcasted_iota(jnp.int32, (16, HD), 0)
    col = lax.broadcasted_iota(jnp.int32, (16, ROWS), 1)
    row = lax.broadcasted_iota(jnp.int32, (16, ROWS), 0)
    parity_ok = (col % 2) == (row // 8)
    lane = lax.broadcasted_iota(jnp.int32, (16, HD), 1)

    def insert(b, r, cache, base_row):
        own = jnp.logical_and(r >= 0, r < SEQ_LOCAL)
        rc = jnp.clip(r, 0, SEQ_LOCAL - 1)
        start = pl.multiple_of((rc // 8) * 16, 16)
        sub = jnp.where(own, rc % 8, -1)
        n0 = kv_s[pl.ds(b * 8 + base_row, 1), :]
        n1 = kv_s[pl.ds(b * 8 + base_row + 1, 1), :]
        new = jnp.where(sub16 % 2 == 0, n0, n1)
        tile = cache[b, pl.ds(start, 16), :].astype(F32)
        cache[b, pl.ds(start, 16), :] = jnp.where(sub16 // 2 == sub, new, tile).astype(BF16)

    def chunk(c, stats):
        kcopy(c).wait()
        vcopy(c).wait()

        for i in range(CB):
            b = c * CB + i
            r = pos[b] - sp * SEQ_LOCAL
            insert(b, r, k_ref, 0)
            insert(b, r, v_ref, 2)
        pltpu.make_async_copy(k_ref.at[pl.ds(c * CB, CB)], k_out.at[pl.ds(c * CB, CB)], kosem.at[c]).start()
        pltpu.make_async_copy(v_ref.at[pl.ds(c * CB, CB)], v_out.at[pl.ds(c * CB, CB)], vosem.at[c]).start()
        scores = []
        for i in range(CB):
            b = c * CB + i
            q = q_s[pl.ds(pl.multiple_of(b * 16, 16), 16), :].astype(BF16)
            scores.append(lax.dot_general(q, k_ref[b], (((1,), (1,)), ((), ())), preferred_element_type=F32) * (HD ** -0.5))
        parts = []
        for i in range(CB):
            r = pos[c * CB + i] - sp * SEQ_LOCAL
            s = jnp.where(jnp.logical_and(parity_ok, col < 2 * r + 2), scores[i], NEG)
            m = jnp.max(s, axis=1, keepdims=True)
            p = jnp.exp(s - m)
            parts.append((m, jnp.sum(p, axis=1, keepdims=True), p.astype(BF16)))
        for i in range(CB):
            b = c * CB + i
            m, l, p = parts[i]
            o_ref[pl.ds(b, 16, stride=NB), :] = jnp.dot(p, v_ref[b], preferred_element_type=F32)
            stats = jnp.where(lane == b, m, jnp.where(lane == b + NB, l, stats))
        return stats

    stats = lax.fori_loop(0, NCB, chunk, jnp.zeros((16, HD), F32))
    for g in range(2):
        block = jnp.concatenate([stats[8 * g:8 * g + 8], jnp.zeros((HD - 8, HD), F32)], axis=0)
        st_ref[g] = jnp.transpose(block).reshape(2, NB, HD)
    for c in range(NCB):
        pltpu.make_async_copy(k_ref.at[pl.ds(c * CB, CB)], k_out.at[pl.ds(c * CB, CB)], kosem.at[c]).wait()
        pltpu.make_async_copy(v_ref.at[pl.ds(c * CB, CB)], v_out.at[pl.ds(c * CB, CB)], vosem.at[c]).wait()


def merge_kernel(o_in, st_in, hid_hbm, w_hbm, out,
                 hid, wbuf, oa, sta, o2, st2, ob, stb, a_own, a_rem, p_s, z1, a_z, z2, t_s, y_in, c_in, cy_in,
                 hsem, wsem, s1, r1, s2, r2, s3, r3, zs, zr, z2s, z2r, ts, ys, yr, cs, cr, cys, cyr):
    dp = lax.axis_index('dp')
    tp = lax.axis_index('tp')
    sp = lax.axis_index('sp')
    core = sp % 2
    yy = sp // 2
    partner = sp + 1 - 2 * core
    ynbr = sp + 2 - 4 * yy
    inner = jnp.logical_or(tp == 1, tp == 2)
    outer = jnp.logical_not(inner)
    n_inner = jnp.where(inner, 1, 0)
    z_in_nbr = jnp.where(tp < 2, jnp.where(tp == 0, 1, 2), jnp.where(tp == 3, 2, 1))
    z_out_nbr = jnp.where(tp < 2, 0, 3)
    nw = jnp.where(core == 1, NW[0], NW[1])
    nc = nw * WPW
    ncp = (NW[0] + NW[1]) * WPW - nc
    cols = jnp.where(core == 1, 0, NW[0] * WC)
    ocols = jnp.where(core == 1, NW[0] * WC, 0)

    def dev(t, s):
        return (dp, t, s)

    barrier = pltpu.get_barrier_semaphore()
    pl.semaphore_signal(barrier, inc=1, device_id=dev(tp, partner), device_id_type=MESH)
    pl.semaphore_signal(barrier, inc=1, device_id=dev(tp, ynbr), device_id_type=MESH)
    pl.semaphore_signal(barrier, inc=1, device_id=dev(z_in_nbr, sp), device_id_type=MESH)

    @pl.when(inner)
    def _():
        pl.semaphore_signal(barrier, inc=1, device_id=dev(z_out_nbr, sp), device_id_type=MESH)

    def wcopy(j):
        return pltpu.make_async_copy(w_hbm.at[:, pl.ds(pl.multiple_of(cols + j * WC, WC), WC)], wbuf.at[j], wsem.at[j])

    def wstart(j, carry):
        wcopy(j).start()
        return carry

    lax.fori_loop(0, nw, wstart, 0)
    hcopy = pltpu.make_async_copy(hid_hbm, hid, hsem)
    hcopy.start()
    pl.semaphore_wait(barrier, 3 + n_inner)

    def rcopy(src, dst, ssem, rsem, t, s):
        return pltpu.make_async_remote_copy(src_ref=src, dst_ref=dst, send_sem=ssem, recv_sem=rsem, device_id=dev(t, s), device_id_type=MESH)

    other = pl.ds(pl.multiple_of((1 - yy) * HALF, HALF), HALF)
    mine = pl.ds(pl.multiple_of(yy * HALF, HALF), HALF)

    cb = rcopy(st_in.at[1 - core], sta, s1.at[NP], r1.at[NP], tp, partner)
    ca = [rcopy(o_in.at[1 - core, pl.ds(i * PIECE, PIECE)], oa.at[pl.ds(i * PIECE, PIECE)], s1.at[i], r1.at[i], tp, partner) for i in range(NP)]
    cb.start()
    for c in ca:
        c.start()
    cd = rcopy(st2.at[:, other, :], stb, s2.at[NP], r2.at[NP], tp, ynbr)
    cc = [rcopy(o2.at[pl.ds(i * PIECE, PIECE), other, :], ob.at[pl.ds(i * PIECE, PIECE)], s2.at[i], r2.at[i], tp, ynbr) for i in range(NP)]
    ce = [rcopy(a_own.at[pl.ds(i * PIECE, PIECE)], a_rem.at[pl.ds(i * PIECE, PIECE)], s3.at[i], r3.at[i], tp, partner) for i in range(NP)]

    def factors(m0, l0, m1, l1):
        top = jnp.maximum(m0, m1)
        f0 = jnp.exp(m0 - top)
        f1 = jnp.exp(m1 - top)
        return top, f0, f1, f0 * l0 + f1 * l1

    def pair_factors(rows):
        top, f0, f1, total = factors(st_in[core, 0, rows, :], st_in[core, 1, rows, :], sta[0, rows, :], sta[1, rows, :])
        st2[0, rows, :] = top
        st2[1, rows, :] = total
        return f0, f1

    def pair_merge(i, rows, f0, f1):
        o2[i, rows, :] = o_in[core, i, rows, :] * f0[:, i:i + 1] + oa[i, rows, :] * f1[:, i:i + 1]

    cb.wait_recv()
    f0, f1 = pair_factors(other)
    cd.start()
    for i in range(NP):
        ca[i].wait_recv()
        for h in range(i * PIECE, (i + 1) * PIECE):
            pair_merge(h, other, f0, f1)
        cc[i].start()
    f0, f1 = pair_factors(mine)
    for h in range(QPK):
        pair_merge(h, mine, f0, f1)
    cd.wait_recv()
    top, f0, f1, total = factors(st2[0, mine, :], st2[1, mine, :], stb[0], stb[1])
    inv = 1.0 / total
    f0 = f0 * inv
    f1 = f1 * inv
    for i in range(NP):
        cc[i].wait_recv()
        for h in range(i * PIECE, (i + 1) * PIECE):
            a = o2[h, mine, :] * f0[:, h:h + 1] + ob[h] * f1[:, h:h + 1]
            a_own[h] = a.astype(BF16).astype(F32)
        ce[i].start()

    def lhs(ref):
        return jnp.concatenate([ref[i].astype(BF16) for i in range(QPK)], axis=1)

    gk = QPK * HD
    own_rows = pl.ds(pl.multiple_of(core * gk, gk), gk)
    rem_rows = pl.ds(pl.multiple_of((1 - core) * gk, gk), gk)
    own = lhs(a_own)

    def first(j, carry):
        wcopy(j).wait()
        p = jnp.dot(own, wbuf[j, own_rows, :], preferred_element_type=F32)
        for e in range(WPW):
            p_s[j * WPW + e] = p[:, e * CW:(e + 1) * CW]
        return carry

    lax.fori_loop(0, nw, first, 0)
    for c in ce:
        c.wait_recv()
    rem = lhs(a_rem)

    def zc(j):
        return rcopy(p_s.at[j], z1.at[j], zs.at[j], zr.at[j], z_in_nbr, sp)

    def second(j, carry):
        p = jnp.dot(rem, wbuf[j, rem_rows, :], preferred_element_type=F32)
        for e in range(WPW):
            p_s[j * WPW + e] += p[:, e * CW:(e + 1) * CW]

        @pl.when(outer)
        def _():
            for e in range(WPW):
                zc(j * WPW + e).start()
        return carry

    lax.fori_loop(0, nw, second, 0)
    hcopy.wait()

    def mid(j):
        return rcopy(a_z.at[j], z2.at[j], z2s.at[j], z2r.at[j], z_in_nbr, sp)

    def back(j):
        return rcopy(t_s.at[j], z1.at[j], ts.at[j], zr.at[j], z_out_nbr, sp)

    def ycopy(src, j):
        return rcopy(src.at[j], y_in.at[j], ys.at[j], yr.at[j], tp, ynbr)

    def ccopy(src, j):
        return rcopy(src.at[j], c_in.at[j], cs.at[j], cr.at[j], tp, partner)

    def cycopy(j):
        return rcopy(y_in.at[j], cy_in.at[j], cys.at[j], cyr.at[j], tp, partner)

    def put(rows_start, col_start, j, val):
        rows = pl.ds(pl.multiple_of(rows_start, HALF), HALF)
        cl = pl.ds(pl.multiple_of(col_start + j * CW, CW), CW)
        out[rows, cl] = (hid[rows, cl].astype(F32) + val).astype(BF16)

    def e3(j):
        ycopy(t_s, j).wait_recv()
        cycopy(j).start()
        put((1 - yy) * HALF, cols, j, y_in[j])

    def e4(j):
        ccopy(t_s, j).wait_recv()
        put(yy * HALF, ocols, j, c_in[j])

    def e5(j):
        cycopy(j).wait_recv()
        put((1 - yy) * HALF, ocols, j, cy_in[j])

    def within(j, n, fn):
        @pl.when(jnp.logical_and(j >= 0, j < n))
        def _():
            fn(j)

    def tail(j, carry):
        e4(j)
        e5(j)
        return carry

    @pl.when(inner)
    def _():
        def e1(j):
            back(j).wait_recv()
            a_z[j] = p_s[j] + z1[j]
            mid(j).start()

        def e2(j):
            mid(j).wait_recv()
            t_s[j] = a_z[j] + z2[j]
            back(j).start()
            ycopy(t_s, j).start()
            ccopy(t_s, j).start()
            put(yy * HALF, cols, j, t_s[j])

        def step(t, carry):
            within(t, nc, e1)
            within(t - SKEW, nc, e2)
            within(t - 2 * SKEW, nc, e3)
            return carry

        lax.fori_loop(0, nc + 2 * SKEW, step, 0)
        lax.fori_loop(0, ncp, tail, 0)

        def drain(j, carry):
            mid(j).wait_send()
            back(j).wait_send()
            ycopy(t_s, j).wait_send()
            ccopy(t_s, j).wait_send()
            cycopy(j).wait_send()
            return carry

        lax.fori_loop(0, nc, drain, 0)

    @pl.when(outer)
    def _():
        def e1(j):
            zc(j).wait_recv()
            ycopy(z1, j).start()
            ccopy(z1, j).start()
            put(yy * HALF, cols, j, z1[j])

        def step(t, carry):
            within(t, nc, e1)
            within(t - SKEW, nc, e3)
            return carry

        lax.fori_loop(0, nc + SKEW, step, 0)
        lax.fori_loop(0, ncp, tail, 0)

        def drain(j, carry):
            zc(j).wait_send()
            ycopy(z1, j).wait_send()
            ccopy(z1, j).wait_send()
            cycopy(j).wait_send()
            return carry

        lax.fori_loop(0, nc, drain, 0)

    for c in ca + cc + ce + [cb, cd]:
        c.wait_send()


def solution(mesh):
    cache_spec = P('dp', 'sp', 'tp', None)
    any_spec = pl.BlockSpec(memory_space=pltpu.HBM)
    vmem_spec = pl.BlockSpec(memory_space=pltpu.VMEM)
    dma = pltpu.SemaphoreType.DMA

    def in_hbm(x):
        return pltpu.with_memory_space_constraint(x, pltpu.HBM)

    def local_step(hidden, norm_scale, w_qkv, w_out, k_cache, v_cache, positions):
        cache_shape = (NB, ROWS, HD)
        cache_out = jax.ShapeDtypeStruct(cache_shape, BF16)
        o, st, k_new, v_new = pl.pallas_call(
            attn_kernel,
            out_shape=(jax.ShapeDtypeStruct((16 * NB, HD), F32), jax.ShapeDtypeStruct((2, 2, NB, HD), F32), cache_out, cache_out),
            in_specs=[any_spec] * 6,
            out_specs=(vmem_spec, vmem_spec, any_spec, any_spec),
            scratch_shapes=[
                pltpu.SMEM((NB,), jnp.int32),
                pltpu.VMEM((D,), BF16),
                pltpu.VMEM((NB, D), BF16),
                pltpu.VMEM((NB, HD), F32),
                pltpu.VMEM((NB, HD), F32),
                pltpu.VMEM((NB, D), BF16),
                pltpu.VMEM((WSLOTS, D, WCOL), BF16),
                pltpu.VMEM((16 * NB, HD), F32),
                pltpu.VMEM((8 * NB, HD), F32),
                pltpu.VMEM(cache_shape, BF16),
                pltpu.VMEM(cache_shape, BF16),
                dma((2,)), dma(()), dma((WSLOTS,)), dma((NCB,)), dma((NCB,)), dma((NCB,)), dma((NCB,)),
            ],
            compiler_params=pltpu.CompilerParams(vmem_limit_bytes=46 << 20),
            name='qkv_attention',
        )(in_hbm(positions), in_hbm(norm_scale), in_hbm(hidden), in_hbm(w_qkv), in_hbm(k_cache.reshape(cache_shape)), in_hbm(v_cache.reshape(cache_shape)))

        chunk = (NC, HALF, CW)
        h_out = pl.pallas_call(
            merge_kernel,
            out_shape=jax.ShapeDtypeStruct((NB, D), BF16),
            in_specs=[vmem_spec, vmem_spec, any_spec, any_spec],
            out_specs=vmem_spec,
            scratch_shapes=[
                pltpu.VMEM((NB, D), BF16),
                pltpu.VMEM((NW[0], 2 * QPK * HD, WC), BF16),
                pltpu.VMEM((QPK, NB, HD), F32),
                pltpu.VMEM((2, NB, HD), F32),
                pltpu.VMEM((QPK, NB, HD), F32),
                pltpu.VMEM((2, NB, HD), F32),
                pltpu.VMEM((QPK, HALF, HD), F32),
                pltpu.VMEM((2, HALF, HD), F32),
                pltpu.VMEM((QPK, HALF, HD), F32),
                pltpu.VMEM((QPK, HALF, HD), F32),
            ] + [pltpu.VMEM(chunk, F32)] * 8 + [
                dma(()), dma((NW[0],)), dma((NP + 1,)), dma((NP + 1,)), dma((NP + 1,)), dma((NP + 1,)), dma((NP,)), dma((NP,)),
            ] + [dma((NC,))] * 11,
            compiler_params=pltpu.CompilerParams(collective_id=0, has_side_effects=True, vmem_limit_bytes=32 << 20),
            name='merge_project',
        )(o.reshape(2, 8, NB, HD), st, in_hbm(hidden), in_hbm(w_out))
        return h_out, k_new.reshape(k_cache.shape), v_new.reshape(v_cache.shape)

    return jax.shard_map(
        local_step,
        mesh=mesh,
        in_specs=(P('dp', None), P(None), P(None, 'tp'), P('tp', None), cache_spec, cache_spec, P('dp')),
        out_specs=(P('dp', None), cache_spec, cache_spec),
        check_vma=False,
    )
```

time: 85 us -> 55 us (0.65)
  local copies, waits for them, and re-layouts: 16.5 us -> 0.88 us
  Pallas kernels: 66.5 us -> 53.3 us
  other arithmetic: 0.95 us -> 0 us
    unnamed x11 -> x1, local copies, waits for them, and re-layouts: 15.8 us -> 0.88 us
    pallas_call x1, Pallas kernels: 28.3 us -> 18.8 us  [local_step(): pl.pallas_call(attn_kernel, out_shape=(jax.ShapeDtypeStruct((16 * NB, HD)...]
    pallas_call x1, Pallas kernels: 38.2 us -> 34.6 us  [local_step(): pl.pallas_call(merge_kernel, out_shape=jax.ShapeDtypeStruct((NB, D), BF16...]
where the time goes in v2:
time: 55 us; the launch traced here: 54.9 us
  Pallas kernels  53.3 us (97%)
  local copies, waits for them, and re-layouts  0.88 us (2%)
  between operations  0.65 us (1%)
    pallas_call x1, Pallas kernels, local_step(): pl.pallas_call(merge_kernel, out_shape=jax.ShapeDtypeStruct((NB, D), BF16...  34.6 us
    pallas_call x1, Pallas kernels, local_step(): pl.pallas_call(attn_kernel, out_shape=(jax.ShapeDtypeStruct((16 * NB, HD)...  18.8 us

profile of v2, /device:TPU:0, one launch (start us, length us, event | category | flops | bytes accessed | tf_op | source)
XLA Modules:
  0.0 54.9 jit_solution(9420506753706369532)
XLA Ops:
  0.6 18.8 %qkv_attention.1 = (f32[1024,128]{1,0:T(8,128)S(1)}, f32[2,2,64,128]{3,2,1,0:T(8,128)S(1)}, bf16[64,512,128]{2,1,0:T(8,128)(2,1)}, bf16[64,512,128]{2,1,0:T(8,128)(2,1)}) custom-call(s32[64]{0:T(128)} %pos_hbm.1, bf16[6144]{0:T(1024)(128)(2,1)} %scale_hbm.1, bf16[64,6144]{1,0:T(8,128)(2,1)} %hid_hbm.3, bf16[6144,2048]{1,0:T(8,128)(2,1)} %w_hbm.2, ...), custom_call_target="tpu_custom_call" | custom-call | tf_op jit(solution)/shard_map/qkv_attention/pallas_call | solution.py:438
  19.4 34.6 %merge_project.1 = bf16[64,6144]{1,0:T(8,128)(2,1)S(1)} custom-call(f32[2,8,64,128]{3,2,1,0:T(8,128)S(1)} %bitcast.5, f32[2,2,64,128]{3,2,1,0:T(8,128)S(1)} %get-tuple-element.8.st_in, bf16[64,6144]{1,0:T(8,128)(2,1)} %hid_hbm.3, bf16[1536,6144]{1,0:T(8,128)(2,1)} %w_hbm.3), custom_call_target="tpu_custom_call" | custom-call | tf_op jit(solution)/shard_map/merge_project/pallas_call | solution.py:462
  54.0 0.9 %copy.11 = bf16[64,6144]{1,0:T(8,128)(2,1)} copy(bf16[64,6144]{1,0:T(8,128)(2,1)S(1)} %merge_project.1) | data formatting | bytes 1572864

commit v3 on v2

--- a/solution.py
+++ b/solution.py
@@ -24,29 +24,32 @@
 NCB = NB // CB
 
 HALF = 32
-CW = 512
+CW = 256
 WC = 512
 NW = (7, 5)
 WPW = WC // CW
 NC = NW[0] * WPW
-SKEW = 2
-PIECE = 2
-NP = QPK // PIECE
+SKEW = 4
+PIECE = 4
 
 
 def attn_kernel(pos_hbm, scale_hbm, hid_hbm, w_hbm, k_hbm, v_hbm,
-                o_ref, st_ref, k_out, v_out,
-                pos, scale, hid, cosf, sinf, x_s, wbuf, q_s, kv_s, k_ref, v_ref, psem, hsem, wsem, ksem, vsem, kosem, vosem):
+                mine_ref, other_ref, k_ref, v_ref,
+                pos, scale, hid, cosf, sinf, x_s, wbuf, q_s, kv_s, psem, hsem, wsem, ksem, vsem):
     sp = lax.axis_index('sp')
+    yy = sp // 2
+
+    def first_of(c):
+        return ((c + (NCB // 2) * (1 - yy)) % NCB) * CB
 
     def wcopy(j):
         return pltpu.make_async_copy(w_hbm.at[:, pl.ds(pl.multiple_of(j * WCOL, WCOL), WCOL)], wbuf.at[j % WSLOTS], wsem.at[j % WSLOTS])
 
     def kcopy(c):
-        return pltpu.make_async_copy(k_hbm.at[pl.ds(c * CB, CB)], k_ref.at[pl.ds(c * CB, CB)], ksem.at[c])
+        return pltpu.make_async_copy(k_hbm.at[pl.ds(first_of(c), CB)], k_ref.at[pl.ds(first_of(c), CB)], ksem.at[c])
 
     def vcopy(c):
-        return pltpu.make_async_copy(v_hbm.at[pl.ds(c * CB, CB)], v_ref.at[pl.ds(c * CB, CB)], vsem.at[c])
+        return pltpu.make_async_copy(v_hbm.at[pl.ds(first_of(c), CB)], v_ref.at[pl.ds(first_of(c), CB)], vsem.at[c])
 
     hcopy = pltpu.make_async_copy(hid_hbm, hid, hsem)
     hcopy.start()
@@ -55,8 +58,9 @@
     scopy = pltpu.make_async_copy(scale_hbm, scale, psem.at[1])
     scopy.start()
     wcopy(0).start()
+    pcopy.wait()
     wcopy(1).start()
-    pcopy.wait()
+    wcopy(2).start()
 
     lane8 = lax.broadcasted_iota(jnp.int32, (8, HD), 1)
     sub8 = lax.broadcasted_iota(jnp.int32, (8, HD), 0)
@@ -75,13 +79,9 @@
 
     lax.fori_loop(0, NB // 8, angle_block, 0)
     q_s[...] = jnp.zeros_like(q_s)
-    wcopy(2).start()
-    wcopy(3).start()
     hcopy.wait()
     scopy.wait()
-    for c in range(2):
-        kcopy(c).start()
-        vcopy(c).start()
+    wcopy(3).start()
 
     def norm_block(i, carry):
         rows = pl.ds(pl.multiple_of(i * 16, 16), 16)
@@ -102,7 +102,7 @@
         for jj in range(4):
             j = g * 4 + jj
             wcopy(j).wait()
-            acc = jnp.dot(x_s[...], wbuf[j % WSLOTS], preferred_element_type=F32)
+            acc = [jnp.dot(x_s[...], wbuf[j % WSLOTS, :, e * HD:(e + 1) * HD], preferred_element_type=F32) for e in range(2)]
 
             @pl.when(g == 0)
             def _():
@@ -110,12 +110,11 @@
 
             @pl.when(g == 1)
             def _():
-                for c in range((2, 4, 5, 6)[jj], (4, 5, 6, 8)[jj]):
+                for c in range((0, 2, 4, 6)[jj], (2, 4, 6, 8)[jj]):
                     kcopy(c).start()
                     vcopy(c).start()
 
-            y = jnp.clip(acc.astype(BF16).astype(F32), -8.0, 8.0)
-            y0, y1 = y[:, :HD], y[:, HD:]
+            y0, y1 = [jnp.clip(y.astype(BF16).astype(F32), -8.0, 8.0) for y in acc]
             if jj < 3:
                 q_s[pl.ds(g * 8 + 2 * jj, NB, stride=16), :] = rope(y0)
                 q_s[pl.ds(g * 8 + 2 * jj + 1, NB, stride=16), :] = rope(y1)
@@ -143,48 +142,58 @@
         tile = cache[b, pl.ds(start, 16), :].astype(F32)
         cache[b, pl.ds(start, 16), :] = jnp.where(sub16 // 2 == sub, new, tile).astype(BF16)
 
-    def chunk(c, stats):
+    def chunk(c, out, m_acc, l_acc):
         kcopy(c).wait()
         vcopy(c).wait()
 
+        b0 = first_of(c)
         for i in range(CB):
-            b = c * CB + i
-            r = pos[b] - sp * SEQ_LOCAL
-            insert(b, r, k_ref, 0)
-            insert(b, r, v_ref, 2)
-        pltpu.make_async_copy(k_ref.at[pl.ds(c * CB, CB)], k_out.at[pl.ds(c * CB, CB)], kosem.at[c]).start()
-        pltpu.make_async_copy(v_ref.at[pl.ds(c * CB, CB)], v_out.at[pl.ds(c * CB, CB)], vosem.at[c]).start()
+            r = pos[b0 + i] - sp * SEQ_LOCAL
+            insert(b0 + i, r, k_ref, 0)
+            insert(b0 + i, r, v_ref, 2)
         scores = []
         for i in range(CB):
-            b = c * CB + i
-            q = q_s[pl.ds(pl.multiple_of(b * 16, 16), 16), :].astype(BF16)
-            scores.append(lax.dot_general(q, k_ref[b], (((1,), (1,)), ((), ())), preferred_element_type=F32) * (HD ** -0.5))
+            q = q_s[pl.ds(pl.multiple_of((b0 + i) * 16, 16), 16), :].astype(BF16)
+            scores.append(lax.dot_general(q, k_ref[b0 + i], (((1,), (1,)), ((), ())), preferred_element_type=F32) * (HD ** -0.5))
         parts = []
         for i in range(CB):
-            r = pos[c * CB + i] - sp * SEQ_LOCAL
+            r = pos[b0 + i] - sp * SEQ_LOCAL
             s = jnp.where(jnp.logical_and(parity_ok, col < 2 * r + 2), scores[i], NEG)
             m = jnp.max(s, axis=1, keepdims=True)
             p = jnp.exp(s - m)
             parts.append((m, jnp.sum(p, axis=1, keepdims=True), p.astype(BF16)))
         for i in range(CB):
-            b = c * CB + i
             m, l, p = parts[i]
-            o_ref[pl.ds(b, 16, stride=NB), :] = jnp.dot(p, v_ref[b], preferred_element_type=F32)
-            stats = jnp.where(lane == b, m, jnp.where(lane == b + NB, l, stats))
-        return stats
-
-    stats = lax.fori_loop(0, NCB, chunk, jnp.zeros((16, HD), F32))
-    for g in range(2):
-        block = jnp.concatenate([stats[8 * g:8 * g + 8], jnp.zeros((HD - 8, HD), F32)], axis=0)
-        st_ref[g] = jnp.transpose(block).reshape(2, NB, HD)
+            o = jnp.dot(p, v_ref[b0 + i], preferred_element_type=F32)
+            bl = (c % (NCB // 2)) * CB + i
+            out[pl.ds(bl, QPK, stride=HALF), :] = o[:QPK]
+            out[pl.ds(QPK * HALF + bl, QPK, stride=HALF), :] = o[8:8 + QPK]
+            m_acc = jnp.where(lane == bl, m, m_acc)
+            l_acc = jnp.where(lane == bl, l, l_acc)
+        return m_acc, l_acc
+
+    for part, out in enumerate((other_ref, mine_ref)):
+        zero = jnp.zeros((16, HD), F32)
+        m_acc, l_acc = lax.fori_loop(part * (NCB // 2), (part + 1) * (NCB // 2), lambda c, st, out=out: chunk(c, out, *st), (zero, zero))
+        block = jnp.concatenate([m_acc, l_acc, jnp.zeros((HD - 32, HD), F32)], axis=0)
+        out[2 * QPK * HALF:(2 * QPK + 1) * HALF, :] = jnp.transpose(block)[:HALF]
+
+
+def write_kernel(k_ref, v_ref, k_out, v_out, sem):
+    copies = []
     for c in range(NCB):
-        pltpu.make_async_copy(k_ref.at[pl.ds(c * CB, CB)], k_out.at[pl.ds(c * CB, CB)], kosem.at[c]).wait()
-        pltpu.make_async_copy(v_ref.at[pl.ds(c * CB, CB)], v_out.at[pl.ds(c * CB, CB)], vosem.at[c]).wait()
-
-
-def merge_kernel(o_in, st_in, hid_hbm, w_hbm, out,
-                 hid, wbuf, oa, sta, o2, st2, ob, stb, a_own, a_rem, p_s, z1, a_z, z2, t_s, y_in, c_in, cy_in,
-                 hsem, wsem, s1, r1, s2, r2, s3, r3, zs, zr, z2s, z2r, ts, ys, yr, cs, cr, cys, cyr):
+        rows = pl.ds(c * CB, CB)
+        copies.append(pltpu.make_async_copy(k_ref.at[rows], k_out.at[rows], sem.at[2 * c]))
+        copies.append(pltpu.make_async_copy(v_ref.at[rows], v_out.at[rows], sem.at[2 * c + 1]))
+    for c in copies:
+        c.start()
+    for c in copies:
+        c.wait()
+
+
+def merge_kernel(mine_in, other_in, hid_hbm, w_hbm, out,
+                 hid, wbuf, om, oc, a_s, p_s, z1, a_z, z2, t_s, y_in, c_in, cy_in,
+                 hsem, wsem, s1, r1, zs, zr, z2s, z2r, ts, ys, yr, cs, cr, cys, cyr):
     dp = lax.axis_index('dp')
     tp = lax.axis_index('tp')
     sp = lax.axis_index('sp')
@@ -225,88 +234,50 @@
     lax.fori_loop(0, nw, wstart, 0)
     hcopy = pltpu.make_async_copy(hid_hbm, hid, hsem)
     hcopy.start()
-    pl.semaphore_wait(barrier, 3 + n_inner)
 
     def rcopy(src, dst, ssem, rsem, t, s):
         return pltpu.make_async_remote_copy(src_ref=src, dst_ref=dst, send_sem=ssem, recv_sem=rsem, device_id=dev(t, s), device_id_type=MESH)
 
-    other = pl.ds(pl.multiple_of((1 - yy) * HALF, HALF), HALF)
-    mine = pl.ds(pl.multiple_of(yy * HALF, HALF), HALF)
-
-    cb = rcopy(st_in.at[1 - core], sta, s1.at[NP], r1.at[NP], tp, partner)
-    ca = [rcopy(o_in.at[1 - core, pl.ds(i * PIECE, PIECE)], oa.at[pl.ds(i * PIECE, PIECE)], s1.at[i], r1.at[i], tp, partner) for i in range(NP)]
-    cb.start()
-    for c in ca:
+    lane = lax.broadcasted_iota(jnp.int32, (HALF, HD), 1)
+    heads = 2 * QPK
+    pieces = [(i * PIECE, PIECE) for i in range(heads // PIECE)] + [(heads, 1)]
+    ca = [rcopy(om.at[pl.ds(i, n)], oc.at[pl.ds(i, n)], s1.at[e], r1.at[e], tp, partner) for e, (i, n) in enumerate(pieces)]
+
+    def factors(x, y):
+        top = jnp.maximum(x, y)
+        f0 = jnp.exp(x - top)
+        f1 = jnp.exp(y - top)
+        return top, f0, f1, f0 * pltpu.roll(x, HD - 16, 1) + f1 * pltpu.roll(y, HD - 16, 1)
+
+    def column(f, h):
+        e = h + 2 * (h // QPK)
+        return f[:, e:e + 1]
+
+    top, f0, f1, total = factors(mine_in[heads], other_in[heads])
+    om[heads] = jnp.where(lane < 16, top, pltpu.roll(total, 16, 1))
+    for h in range(heads):
+        om[h] = mine_in[h] * column(f0, h) + other_in[h] * column(f1, h)
+    pl.semaphore_wait(barrier, 3 + n_inner)
+    for c in ca[::-1]:
         c.start()
-    cd = rcopy(st2.at[:, other, :], stb, s2.at[NP], r2.at[NP], tp, ynbr)
-    cc = [rcopy(o2.at[pl.ds(i * PIECE, PIECE), other, :], ob.at[pl.ds(i * PIECE, PIECE)], s2.at[i], r2.at[i], tp, ynbr) for i in range(NP)]
-    ce = [rcopy(a_own.at[pl.ds(i * PIECE, PIECE)], a_rem.at[pl.ds(i * PIECE, PIECE)], s3.at[i], r3.at[i], tp, partner) for i in range(NP)]
-
-    def factors(m0, l0, m1, l1):
-        top = jnp.maximum(m0, m1)
-        f0 = jnp.exp(m0 - top)
-        f1 = jnp.exp(m1 - top)
-        return top, f0, f1, f0 * l0 + f1 * l1
-
-    def pair_factors(rows):
-        top, f0, f1, total = factors(st_in[core, 0, rows, :], st_in[core, 1, rows, :], sta[0, rows, :], sta[1, rows, :])
-        st2[0, rows, :] = top
-        st2[1, rows, :] = total
-        return f0, f1
-
-    def pair_merge(i, rows, f0, f1):
-        o2[i, rows, :] = o_in[core, i, rows, :] * f0[:, i:i + 1] + oa[i, rows, :] * f1[:, i:i + 1]
-
-    cb.wait_recv()
-    f0, f1 = pair_factors(other)
-    cd.start()
-    for i in range(NP):
-        ca[i].wait_recv()
-        for h in range(i * PIECE, (i + 1) * PIECE):
-            pair_merge(h, other, f0, f1)
-        cc[i].start()
-    f0, f1 = pair_factors(mine)
-    for h in range(QPK):
-        pair_merge(h, mine, f0, f1)
-    cd.wait_recv()
-    top, f0, f1, total = factors(st2[0, mine, :], st2[1, mine, :], stb[0], stb[1])
+    ca[-1].wait_recv()
+    top, f0, f1, total = factors(om[heads], oc[heads])
     inv = 1.0 / total
     f0 = f0 * inv
     f1 = f1 * inv
-    for i in range(NP):
-        cc[i].wait_recv()
-        for h in range(i * PIECE, (i + 1) * PIECE):
-            a = o2[h, mine, :] * f0[:, h:h + 1] + ob[h] * f1[:, h:h + 1]
-            a_own[h] = a.astype(BF16).astype(F32)
-        ce[i].start()
-
-    def lhs(ref):
-        return jnp.concatenate([ref[i].astype(BF16) for i in range(QPK)], axis=1)
-
-    gk = QPK * HD
-    own_rows = pl.ds(pl.multiple_of(core * gk, gk), gk)
-    rem_rows = pl.ds(pl.multiple_of((1 - core) * gk, gk), gk)
-    own = lhs(a_own)
-
-    def first(j, carry):
-        wcopy(j).wait()
-        p = jnp.dot(own, wbuf[j, own_rows, :], preferred_element_type=F32)
-        for e in range(WPW):
-            p_s[j * WPW + e] = p[:, e * CW:(e + 1) * CW]
-        return carry
-
-    lax.fori_loop(0, nw, first, 0)
-    for c in ce:
-        c.wait_recv()
-    rem = lhs(a_rem)
+    for e, (i, n) in reversed(list(enumerate(pieces[:-1]))):
+        ca[e].wait_recv()
+        for h in range(i, i + n):
+            a_s[:, h * HD:(h + 1) * HD] = (om[h] * column(f0, h) + oc[h] * column(f1, h)).astype(BF16)
 
     def zc(j):
         return rcopy(p_s.at[j], z1.at[j], zs.at[j], zr.at[j], z_in_nbr, sp)
 
-    def second(j, carry):
-        p = jnp.dot(rem, wbuf[j, rem_rows, :], preferred_element_type=F32)
-        for e in range(WPW):
-            p_s[j * WPW + e] += p[:, e * CW:(e + 1) * CW]
+    def project(j, carry):
+        wcopy(j).wait()
+        for e in range(WC // 128):
+            p = jnp.dot(a_s[...], wbuf[j, :, e * 128:(e + 1) * 128], preferred_element_type=F32)
+            p_s[j * WPW + e * 128 // CW, :, (e * 128) % CW:(e * 128) % CW + 128] = p
 
         @pl.when(outer)
         def _():
@@ -314,7 +285,7 @@
                 zc(j * WPW + e).start()
         return carry
 
-    lax.fori_loop(0, nw, second, 0)
+    lax.fori_loop(0, nw, project, 0)
     hcopy.wait()
 
     def mid(j):
@@ -419,7 +390,7 @@
 
         lax.fori_loop(0, nc, drain, 0)
 
-    for c in ca + cc + ce + [cb, cd]:
+    for c in ca:
         c.wait_send()
 
 
@@ -435,11 +406,13 @@
     def local_step(hidden, norm_scale, w_qkv, w_out, k_cache, v_cache, positions):
         cache_shape = (NB, ROWS, HD)
         cache_out = jax.ShapeDtypeStruct(cache_shape, BF16)
-        o, st, k_new, v_new = pl.pallas_call(
+        part = jax.ShapeDtypeStruct(((2 * QPK + 1) * HALF, HD), F32)
+        cache_vmem = pltpu.VMEM(cache_shape, BF16)
+        mine, other, k_vmem, v_vmem = pl.pallas_call(
             attn_kernel,
-            out_shape=(jax.ShapeDtypeStruct((16 * NB, HD), F32), jax.ShapeDtypeStruct((2, 2, NB, HD), F32), cache_out, cache_out),
+            out_shape=(part, part, cache_vmem, cache_vmem),
             in_specs=[any_spec] * 6,
-            out_specs=(vmem_spec, vmem_spec, any_spec, any_spec),
+            out_specs=(vmem_spec,) * 4,
             scratch_shapes=[
                 pltpu.SMEM((NB,), jnp.int32),
                 pltpu.VMEM((D,), BF16),
@@ -450,14 +423,26 @@
                 pltpu.VMEM((WSLOTS, D, WCOL), BF16),
                 pltpu.VMEM((16 * NB, HD), F32),
                 pltpu.VMEM((8 * NB, HD), F32),
-                pltpu.VMEM(cache_shape, BF16),
-                pltpu.VMEM(cache_shape, BF16),
-                dma((2,)), dma(()), dma((WSLOTS,)), dma((NCB,)), dma((NCB,)), dma((NCB,)), dma((NCB,)),
+                dma((2,)), dma(()), dma((WSLOTS,)), dma((NCB,)), dma((NCB,)),
             ],
-            compiler_params=pltpu.CompilerParams(vmem_limit_bytes=46 << 20),
+            compiler_params=pltpu.CompilerParams(vmem_limit_bytes=24 << 20),
             name='qkv_attention',
         )(in_hbm(positions), in_hbm(norm_scale), in_hbm(hidden), in_hbm(w_qkv), in_hbm(k_cache.reshape(cache_shape)), in_hbm(v_cache.reshape(cache_shape)))
 
+        sps = mesh.shape['sp']
+        other = lax.ppermute(other, 'sp', [(i, (i + sps // 2) % sps) for i in range(sps)])
+        k_new, v_new = pl.pallas_call(
+            write_kernel,
+            out_shape=(cache_out, cache_out),
+            in_specs=[vmem_spec] * 2,
+            out_specs=(any_spec,) * 2,
+            scratch_shapes=[dma((2 * NCB,))],
+            compiler_params=pltpu.CompilerParams(vmem_limit_bytes=4 << 20),
+            cost_estimate=pl.CostEstimate(flops=20_000_000_000, bytes_accessed=32 << 20, transcendentals=0),
+            name='cache_write',
+        )(k_vmem, v_vmem)
+
+        heads = (2 * QPK + 1, HALF, HD)
         chunk = (NC, HALF, CW)
         h_out = pl.pallas_call(
             merge_kernel,
@@ -467,20 +452,15 @@
             scratch_shapes=[
                 pltpu.VMEM((NB, D), BF16),
                 pltpu.VMEM((NW[0], 2 * QPK * HD, WC), BF16),
-                pltpu.VMEM((QPK, NB, HD), F32),
-                pltpu.VMEM((2, NB, HD), F32),
-                pltpu.VMEM((QPK, NB, HD), F32),
-                pltpu.VMEM((2, NB, HD), F32),
-                pltpu.VMEM((QPK, HALF, HD), F32),
-                pltpu.VMEM((2, HALF, HD), F32),
-                pltpu.VMEM((QPK, HALF, HD), F32),
-                pltpu.VMEM((QPK, HALF, HD), F32),
+                pltpu.VMEM(heads, F32),
+                pltpu.VMEM(heads, F32),
+                pltpu.VMEM((HALF, 2 * QPK * HD), BF16),
             ] + [pltpu.VMEM(chunk, F32)] * 8 + [
-                dma(()), dma((NW[0],)), dma((NP + 1,)), dma((NP + 1,)), dma((NP + 1,)), dma((NP + 1,)), dma((NP,)), dma((NP,)),
+                dma(()), dma((NW[0],)), dma((2 * QPK // PIECE + 1,)), dma((2 * QPK // PIECE + 1,)),
             ] + [dma((NC,))] * 11,
             compiler_params=pltpu.CompilerParams(collective_id=0, has_side_effects=True, vmem_limit_bytes=32 << 20),
             name='merge_project',
-        )(o.reshape(2, 8, NB, HD), st, in_hbm(hidden), in_hbm(w_out))
+        )(mine.reshape(heads), other.reshape(heads), in_hbm(hidden), in_hbm(w_out))
         return h_out, k_new.reshape(k_cache.shape), v_new.reshape(v_cache.shape)
 
     return jax.shard_map(

time: 55 us -> 50.9 us (0.925)
  Pallas kernels: 53.3 us -> 46.1 us
  starting transfers between devices: 0 us -> 3.1 us
    pallas_call x1, Pallas kernels: 34.6 us -> 25.1 us  [local_step(): pl.pallas_call(merge_kernel, out_shape=jax.ShapeDtypeStruct((NB, D), BF16...]
    ppermute x0 -> x1, starting transfers between devices: none -> 3.1 us  [local_step(): lax.ppermute(other, 'sp', [(i, (i + sps // 2) % sps) for i in range(sps)])]
    pallas_call x1 -> x2, Pallas kernels: 18.8 us -> 21 us  [the longest x1 15 us: local_step(): pl.pallas_call(attn_kernel, out_shape=(part, part, cache_vmem, cache_vmem...]
  transfers between devices with their start and end apart: 0 -> 1, of which waited for: 0 -> 0; matrix products, arithmetic and copies ran while one was open for 0% -> 0% of each run, Pallas kernels for 0% -> 12%
where the time goes in v3:
time: 50.9 us; the launch traced here: 50.8 us
  Pallas kernels  46.1 us (91%)
  starting transfers between devices  3.1 us (6%)
  local copies, waits for them, and re-layouts  0.88 us (2%)
  between operations  0.66 us (1%)
    pallas_call x1, Pallas kernels, local_step(): pl.pallas_call(merge_kernel, out_shape=jax.ShapeDtypeStruct((NB, D), BF16...  25.1 us
    pallas_call x1, Pallas kernels, local_step(): pl.pallas_call(attn_kernel, out_shape=(part, part, cache_vmem, cache_vmem...  15 us
    pallas_call x1, Pallas kernels, local_step(): pl.pallas_call(write_kernel, out_shape=(cache_out, cache_out), in_specs=[...  5.96 us
    ppermute x1, starting transfers between devices, local_step(): lax.ppermute(other, 'sp', [(i, (i + sps // 2) % sps) for i in range(sps)])  3.1 us
  transfers between devices with their start and end apart: 1, of which 0 were waited for; matrix products, arithmetic and copies ran while one was open for 0% of the time, Pallas kernels for 12%

profile of v3, /device:TPU:0, one launch (start us, length us, event | category | flops | bytes accessed | tf_op | source)
XLA Modules:
  0.0 50.8 jit_solution(2257619060139437034)
XLA Ops:
  0.6 15.0 %qkv_attention.1 = (f32[416,128]{1,0:T(8,128)S(1)}, f32[416,128]{1,0:T(8,128)S(1)}, bf16[64,512,128]{2,1,0:T(8,128)(2,1)S(1)}, bf16[64,512,128]{2,1,0:T(8,128)(2,1)S(1)}) custom-call(s32[64]{0:T(128)} %pos_hbm.1, bf16[6144]{0:T(1024)(128)(2,1)} %scale_hbm.1, bf16[64,6144]{1,0:T(8,128)(2,1)} %hid_hbm.3, bf16[6144,2048]{1,0:T(8,128)(2,1)} %w_hbm.2, ...), custom_call_target="tpu_custom_call" | custom-call | tf_op jit(solution)/shard_map/qkv_attention/pallas_call | solution.py:411
  15.7 3.1 %collective-permute-start = (f32[416,128]{1,0:T(8,128)S(1)}, f32[416,128]{1,0:T(8,128)S(1)}, u32[]{:S(2)}, u32[]{:S(2)}) collective-permute-start(f32[416,128]{1,0:T(8,128)S(1)} %get-tuple-element.10), channel_id=1, source_target_pairs={{0,2},{1,3},{2,0},{3,1},{4,6},{5,7},{6,4},{7,5},{8,10},{9,11},{10,... | collective-permute-start | bytes 638984 | tf_op jit(solution)/shard_map/ppermute | solution.py:433
  18.8 6.0 %cache_write.1 = (bf16[64,512,128]{2,1,0:T(8,128)(2,1)}, bf16[64,512,128]{2,1,0:T(8,128)(2,1)}) custom-call(bf16[64,512,128]{2,1,0:T(8,128)(2,1)S(1)} %get-tuple-element.11.k_ref, bf16[64,512,128]{2,1,0:T(8,128)(2,1)S(1)} %get-tuple-element.12.v_ref), custom_call_target="tpu_custom_call" | custom-call | flops 20000000000 | bytes 33554432 | tf_op jit(solution)/shard_map/cache_write/pallas_call | solution.py:434
  24.7 0.0 collective-permute-done
  24.8 25.1 %merge_project.1 = bf16[64,6144]{1,0:T(8,128)(2,1)S(1)} custom-call(f32[13,32,128]{2,1,0:T(8,128)S(1)} %bitcast.6, f32[13,32,128]{2,1,0:T(8,128)S(1)} %bitcast.7, bf16[64,6144]{1,0:T(8,128)(2,1)} %hid_hbm.3, bf16[1536,6144]{1,0:T(8,128)(2,1)} %w_hbm.3), custom_call_target="tpu_custom_call" | custom-call | tf_op jit(solution)/shard_map/merge_project/pallas_call | solution.py:447
  49.9 0.9 %copy.11 = bf16[64,6144]{1,0:T(8,128)(2,1)} copy(bf16[64,6144]{1,0:T(8,128)(2,1)S(1)} %merge_project.1) | data formatting | bytes 1572864
Async XLA Ops:
  15.7 9.1 %collective-permute-start = (f32[416,128]{1,0:T(8,128)S(1)}, f32[416,128]{1,0:T(8,128)S(1)}, u32[]{:S(2)}, u32[]{:S(2)}) collective-permute-start(f32[416,128]{1,0:T(8,128)S(1)} %get-tuple-element.10), channel_id=1, source_target_pairs={{0,2},{1,3},{2,0},{3,1},{4,6},{5,7},{6,4},{7,5},{8,10},{9,11},{10,... | collective-permute-start | bytes 638984 | tf_op jit(solution)/shard_map/ppermute | solution.py:433

commit v4 on v3

--- a/solution.py
+++ b/solution.py
@@ -20,7 +20,7 @@
 
 WCOL = 256
 WSLOTS = 4
-CB = 8
+CB = 16
 NCB = NB // CB
 
 HALF = 32
@@ -110,7 +110,7 @@
 
             @pl.when(g == 1)
             def _():
-                for c in range((0, 2, 4, 6)[jj], (2, 4, 6, 8)[jj]):
+                for c in range((0, 1, 2, 3)[jj], (1, 2, 3, 4)[jj]):
                     kcopy(c).start()
                     vcopy(c).start()
 

time: 50.9 us -> 50.7 us (level)
  no operation moved by 1% of the time
where the time goes in v4:
time: 50.7 us; the launch traced here: 50.6 us
  Pallas kernels  45.9 us (91%)
  starting transfers between devices  3.09 us (6%)
  local copies, waits for them, and re-layouts  0.88 us (2%)
  between operations  0.66 us (1%)
    pallas_call x1, Pallas kernels, local_step(): pl.pallas_call(merge_kernel, out_shape=jax.ShapeDtypeStruct((NB, D), BF16...  25.2 us
    pallas_call x1, Pallas kernels, local_step(): pl.pallas_call(attn_kernel, out_shape=(part, part, cache_vmem, cache_vmem...  14.8 us
    pallas_call x1, Pallas kernels, local_step(): pl.pallas_call(write_kernel, out_shape=(cache_out, cache_out), in_specs=[...  5.92 us
    ppermute x1, starting transfers between devices, local_step(): lax.ppermute(other, 'sp', [(i, (i + sps // 2) % sps) for i in range(sps)])  3.09 us
  transfers between devices with their start and end apart: 1, of which 0 were waited for; matrix products, arithmetic and copies ran while one was open for 0% of the time, Pallas kernels for 12%

profile of v4, /device:TPU:0, one launch (start us, length us, event | category | flops | bytes accessed | tf_op | source)
XLA Modules:
  0.0 50.6 jit_solution(7333712736584633112)
XLA Ops:
  0.6 14.8 %qkv_attention.1 = (f32[416,128]{1,0:T(8,128)S(1)}, f32[416,128]{1,0:T(8,128)S(1)}, bf16[64,512,128]{2,1,0:T(8,128)(2,1)S(1)}, bf16[64,512,128]{2,1,0:T(8,128)(2,1)S(1)}) custom-call(s32[64]{0:T(128)} %pos_hbm.1, bf16[6144]{0:T(1024)(128)(2,1)} %scale_hbm.1, bf16[64,6144]{1,0:T(8,128)(2,1)} %hid_hbm.3, bf16[6144,2048]{1,0:T(8,128)(2,1)} %w_hbm.2, ...), custom_call_target="tpu_custom_call" | custom-call | tf_op jit(solution)/shard_map/qkv_attention/pallas_call | solution.py:411
  15.5 3.1 %collective-permute-start = (f32[416,128]{1,0:T(8,128)S(1)}, f32[416,128]{1,0:T(8,128)S(1)}, u32[]{:S(2)}, u32[]{:S(2)}) collective-permute-start(f32[416,128]{1,0:T(8,128)S(1)} %get-tuple-element.10), channel_id=1, source_target_pairs={{0,2},{1,3},{2,0},{3,1},{4,6},{5,7},{6,4},{7,5},{8,10},{9,11},{10,... | collective-permute-start | bytes 638984 | tf_op jit(solution)/shard_map/ppermute | solution.py:433
  18.5 5.9 %cache_write.1 = (bf16[64,512,128]{2,1,0:T(8,128)(2,1)}, bf16[64,512,128]{2,1,0:T(8,128)(2,1)}) custom-call(bf16[64,512,128]{2,1,0:T(8,128)(2,1)S(1)} %get-tuple-element.11.k_ref, bf16[64,512,128]{2,1,0:T(8,128)(2,1)S(1)} %get-tuple-element.12.v_ref), custom_call_target="tpu_custom_call" | custom-call | flops 20000000000 | bytes 33554432 | tf_op jit(solution)/shard_map/cache_write/pallas_call | solution.py:434
  24.5 0.0 collective-permute-done
  24.5 25.2 %merge_project.1 = bf16[64,6144]{1,0:T(8,128)(2,1)S(1)} custom-call(f32[13,32,128]{2,1,0:T(8,128)S(1)} %bitcast.6, f32[13,32,128]{2,1,0:T(8,128)S(1)} %bitcast.7, bf16[64,6144]{1,0:T(8,128)(2,1)} %hid_hbm.3, bf16[1536,6144]{1,0:T(8,128)(2,1)} %w_hbm.3), custom_call_target="tpu_custom_call" | custom-call | tf_op jit(solution)/shard_map/merge_project/pallas_call | solution.py:447
  49.7 0.9 %copy.11 = bf16[64,6144]{1,0:T(8,128)(2,1)} copy(bf16[64,6144]{1,0:T(8,128)(2,1)S(1)} %merge_project.1) | data formatting | bytes 1572864
Async XLA Ops:
  15.5 9.0 %collective-permute-start = (f32[416,128]{1,0:T(8,128)S(1)}, f32[416,128]{1,0:T(8,128)S(1)}, u32[]{:S(2)}, u32[]{:S(2)}) collective-permute-start(f32[416,128]{1,0:T(8,128)S(1)} %get-tuple-element.10), channel_id=1, source_target_pairs={{0,2},{1,3},{2,0},{3,1},{4,6},{5,7},{6,4},{7,5},{8,10},{9,11},{10,... | collective-permute-start | bytes 638984 | tf_op jit(solution)/shard_map/ppermute | solution.py:433
